TPU v7x, 8 devices: a whole 2x2x1 slice. The times are simulated.
8 devices in a mesh: local: 2 (over z, y), data: 4 (over x, core).
Axes of the slice: x: 2, y: 2, z: 1, core: 2. Of those that a mesh axis runs over, the one named last changes fastest.
Arguments:
- x_in: bfloat16 [32768, 1280], P(('local', 'data'))
- grad_out: bfloat16 [32768, 1280], P(('local', 'data'))
- w_in: bfloat16 [3, 1280, 5120], P(None, ('local', 'data'))
- w_out: bfloat16 [3, 5120, 1280], P(None, ('local', 'data'))
Outputs:
- output 1: bfloat16 [32768, 1280], P(('local', 'data'))
- output 2: float32 [3, 1280, 5120], P(None, ('local', 'data'))
- output 3: float32 [3, 5120, 1280], P(None, ('local', 'data'))
- output 4: bfloat16 [32768, 1280], P(('local', 'data'))
All inputs are finite; a program needn't handle non-finite values.
Results may differ from a plain program's by a relative error of at most 0.0166592.
Values are sent between devices in bfloat16 or wider.
A program may use at most 1 GiB of HBM per device.

v0:
```python
import jax
import jax.numpy as jnp
from jax import lax
from jax.sharding import PartitionSpec as P, NamedSharding

NORM_EPS = 1e-6
LAST_LAST = (((1,), (1,)), ((), ()))
FIRST_FIRST = (((0,), (0,)), ((), ()))


def norm_rows(x_rows):
    x_wide = x_rows.astype(jnp.float32)
    inv_rms = lax.rsqrt(jnp.mean(x_wide * x_wide, axis=-1, keepdims=True) + NORM_EPS)
    return x_wide * inv_rms, inv_rms


def layer_forward(x_rows, w_in, w_out):
    unit_rows = norm_rows(x_rows)[0].astype(jnp.bfloat16)
    pre_act = jnp.dot(unit_rows, w_in, preferred_element_type=jnp.float32).astype(jnp.bfloat16)
    hidden = jax.nn.gelu(pre_act.astype(jnp.float32)).astype(jnp.bfloat16)
    branch = jnp.dot(hidden, w_out, preferred_element_type=jnp.float32)
    return (x_rows.astype(jnp.float32) + branch).astype(jnp.bfloat16)


def layer_backward(x_rows, grad_rows, w_in, w_out):
    unit_wide, inv_rms = norm_rows(x_rows)
    unit_rows = unit_wide.astype(jnp.bfloat16)
    pre_act = jnp.dot(unit_rows, w_in, preferred_element_type=jnp.float32).astype(jnp.bfloat16)
    gelu_val, gelu_back = jax.vjp(jax.nn.gelu, pre_act.astype(jnp.float32))
    hidden = gelu_val.astype(jnp.bfloat16)
    grad_hidden = lax.dot_general(grad_rows, w_out, LAST_LAST, preferred_element_type=jnp.float32)
    grad_pre = gelu_back(grad_hidden)[0].astype(jnp.bfloat16)
    grad_w_out = lax.dot_general(hidden, grad_rows, FIRST_FIRST, preferred_element_type=jnp.float32)
    grad_w_in = lax.dot_general(unit_rows, grad_pre, FIRST_FIRST, preferred_element_type=jnp.float32)
    grad_unit = lax.dot_general(grad_pre, w_in, LAST_LAST, preferred_element_type=jnp.float32)
    row_mean = jnp.mean(grad_unit * unit_wide, axis=-1, keepdims=True)
    grad_x = grad_rows.astype(jnp.float32) + inv_rms * (grad_unit - unit_wide * row_mean)
    return grad_x.astype(jnp.bfloat16), grad_w_in, grad_w_out


def solution(mesh):
    row_spec = P(('local', 'data'), None)
    weight_spec = P(None, ('local', 'data'), None)

    def device_step(x_rows, grad_rows, w_in_part, w_out_part):
        layers = w_in_part.shape[0]
        saved_x = []
        kept_in = []
        kept_out = []
        x_cur = x_rows
        for layer_idx in range(layers):
            sub_in = lax.all_gather(w_in_part[layer_idx], 'data', axis=0, tiled=True)
            sub_out = lax.all_gather(w_out_part[layer_idx], 'data', axis=0, tiled=True)
            full_in = lax.all_gather(sub_in, 'local', axis=0, tiled=True)
            full_out = lax.all_gather(sub_out, 'local', axis=0, tiled=True)
            saved_x.append(x_cur)
            kept_in.append(sub_in)
            kept_out.append(sub_out)
            x_cur = layer_forward(x_cur, full_in, full_out)
        grad_cur = grad_rows
        grads_in = []
        grads_out = []
        for layer_idx in reversed(range(layers)):
            sub_in, sub_out, grad_cur = lax.optimization_barrier((kept_in[layer_idx], kept_out[layer_idx], grad_cur))
            full_in = lax.all_gather(sub_in, 'local', axis=0, tiled=True)
            full_out = lax.all_gather(sub_out, 'local', axis=0, tiled=True)
            grad_cur, part_in, part_out = layer_backward(saved_x[layer_idx], grad_cur, full_in, full_out)
            grads_in.append(lax.psum_scatter(part_in, ('local', 'data'), scatter_dimension=0, tiled=True))
            grads_out.append(lax.psum_scatter(part_out, ('local', 'data'), scatter_dimension=0, tiled=True))
        return x_cur, jnp.stack(grads_in[::-1]), jnp.stack(grads_out[::-1]), grad_cur

    return jax.shard_map(device_step, mesh=mesh, in_specs=(row_spec, row_spec, weight_spec, weight_spec), out_specs=(row_spec, weight_spec, weight_spec, row_spec), check_vma=False)
```

profile of v0, /device:TPU:0, one launch (start us, length us, event | category | flops | bytes accessed | tf_op | source)
XLA Modules:
  0.0 3531.6 jit_solution(1959991896518406280)
XLA Ops:
  7.2 4.8 fusion.156
  12.0 0.0 all-gather.47.cloned.1.call-start
  12.1 4.8 fusion.157
  16.9 0.7 all-gather.51.cloned.1.call-update
  17.6 0.5 all-gather.55.cloned.1.call-update
  18.2 0.5 all-gather.59.cloned.1.call-update
  18.8 0.5 all-gather.63.cloned.1.call-update
  19.4 40.7 %all-gather.43.cloned.1.call-done = bf16[1,640,5120]{2,1,0:T(8,128)(2,1)} async-done(((bf16[1,160,5120]{2,1,0:T(8,128)(2,1)}), bf16[1,640,5120]{2,1,0:T(8,128)(2,1)}) %all-gather.43.cloned.1.call-update) | async-done | bytes 6553616 | tf_op jit(solution)/shard_map/all_gather | solution.py:52
  60.2 47.2 %all-gather.47.cloned.1.call-done = bf16[1,2560,1280]{2,1,0:T(8,128)(2,1)} async-done(((bf16[1,640,1280]{2,1,0:T(8,128)(2,1)}), bf16[1,2560,1280]{2,1,0:T(8,128)(2,1)}) %all-gather.47.cloned.1.call-update) | async-done | bytes 6553616 | tf_op jit(solution)/shard_map/all_gather | solution.py:53
  107.5 46.6 %all-gather.51.cloned.1.call-done = bf16[1,640,5120]{2,1,0:T(8,128)(2,1)} async-done(((bf16[1,160,5120]{2,1,0:T(8,128)(2,1)}), bf16[1,640,5120]{2,1,0:T(8,128)(2,1)}) %all-gather.51.cloned.1.call-update) | async-done | bytes 6553616 | tf_op jit(solution)/shard_map/all_gather | solution.py:52
  154.2 47.0 %all-gather.55.cloned.1.call-done = bf16[1,2560,1280]{2,1,0:T(8,128)(2,1)} async-done(((bf16[1,640,1280]{2,1,0:T(8,128)(2,1)}), bf16[1,2560,1280]{2,1,0:T(8,128)(2,1)}) %all-gather.55.cloned.1.call-update) | async-done | bytes 6553616 | tf_op jit(solution)/shard_map/all_gather | solution.py:53
  201.3 47.0 %all-gather.59.cloned.1.call-done = bf16[1,640,5120]{2,1,0:T(8,128)(2,1)} async-done(((bf16[1,160,5120]{2,1,0:T(8,128)(2,1)}), bf16[1,640,5120]{2,1,0:T(8,128)(2,1)}) %all-gather.59.cloned.1.call-update) | async-done | bytes 6553616 | tf_op jit(solution)/shard_map/all_gather | solution.py:52
  248.3 47.1 %all-gather.63.cloned.1.call-done = bf16[1,2560,1280]{2,1,0:T(8,128)(2,1)} async-done(((bf16[1,640,1280]{2,1,0:T(8,128)(2,1)}), bf16[1,2560,1280]{2,1,0:T(8,128)(2,1)}) %all-gather.63.cloned.1.call-update) | async-done | bytes 6553616 | tf_op jit(solution)/shard_map/all_gather | solution.py:53
  295.5 14.3 copy.8
  309.8 6.1 fusion.84
  315.9 14.3 copy.10
  330.2 0.2 all-gather.37.cloned.1.call-start
  330.5 122.8 %all-gather.45.cloned.1.call-done = bf16[1,1280,5120]{2,1,0:T(8,128)(2,1)} async-done(((bf16[1,640,5120]{2,1,0:T(8,128)(2,1)}), bf16[1,1280,5120]{2,1,0:T(8,128)(2,1)}) %all-gather.45.cloned.1.call-update) | async-done | bytes 13107216 | tf_op jit(solution)/shard_map/all_gather | solution.py:54
  453.3 85.0 %fusion.91.clone.4 = bf16[4096,5120]{1,0:T(8,128)(2,1)} fusion(bf16[1,1280,5120]{2,1,0:T(8,128)(2,1)} %all-gather.45.cloned.1.call-done, bf16[4096,1280]{0,1:T(8,128)(2,1)} %copy.8, f32[4096]{0:T(1024)S(1)} %add_rsqrt_fusion.2), kind=kOutput, calls=%fused_computation.44.clone.clone.clone.clone.clone.clone.1 | convolution fusion | flops 53933506560 | bytes 65552384 | tf_op jit(solution)/shard_map/dot_general | solution.py:19
  538.3 72.9 %all-gather.49.cloned.1.call-done = bf16[1,5120,1280]{2,1,0:T(8,128)(2,1)} async-done(((bf16[1,2560,1280]{2,1,0:T(8,128)(2,1)}), bf16[1,5120,1280]{2,1,0:T(8,128)(2,1)}) %all-gather.49.cloned.1.call-update) | async-done | bytes 13107216 | tf_op jit(solution)/shard_map/all_gather | solution.py:55
  611.2 90.6 %fusion.86 = (f32[4096]{0:T(1024)S(1)}, bf16[4096,1280]{0,1:T(8,128)(2,1)}) fusion(bf16[1,5120,1280]{2,1,0:T(8,128)(2,1)} %all-gather.49.cloned.1.call-done, bf16[4096,1280]{0,1:T(8,128)(2,1)} %copy.8, bf16[4096,5120]{1,0:T(8,128)(2,1)} %fusion.91.clone.4), kind=kOutput, calls=%fused_computation.119 | convolution fusion | flops 53718544384 | bytes 76038144 | tf_op jit(solution)/shard_map/dot_general | solution.py:21
  701.8 67.2 %all-gather.53.cloned.1.call-done = bf16[1,1280,5120]{2,1,0:T(8,128)(2,1)} async-done(((bf16[1,640,5120]{2,1,0:T(8,128)(2,1)}), bf16[1,1280,5120]{2,1,0:T(8,128)(2,1)}) %all-gather.53.cloned.1.call-update) | async-done | bytes 13107216 | tf_op jit(solution)/shard_map/all_gather | solution.py:54
  769.1 85.0 %fusion.93.clone.2 = bf16[4096,5120]{1,0:T(8,128)(2,1)} fusion(bf16[1,1280,5120]{2,1,0:T(8,128)(2,1)} %all-gather.53.cloned.1.call-done, bf16[4096,1280]{0,1:T(8,128)(2,1)} %get-tuple-element.33, f32[4096]{0:T(1024)S(1)} %add_rsqrt_fusion.1), kind=kOutput, calls=%fused_computation.50.clone.clone.clone.clone.clone.clone | convolution fusion | flops 53933506560 | bytes 65552384 | tf_op jit(solution)/shard_map/dot_general | solution.py:19
  854.0 72.7 %all-gather.57.cloned.1.call-done = bf16[1,5120,1280]{2,1,0:T(8,128)(2,1)} async-done(((bf16[1,2560,1280]{2,1,0:T(8,128)(2,1)}), bf16[1,5120,1280]{2,1,0:T(8,128)(2,1)}) %all-gather.57.cloned.1.call-update) | async-done | bytes 13107216 | tf_op jit(solution)/shard_map/all_gather | solution.py:55
  926.8 90.9 %fusion.88 = (f32[4096]{0:T(1024)S(1)}, bf16[4096,1280]{0,1:T(8,128)(2,1)}) fusion(bf16[1,5120,1280]{2,1,0:T(8,128)(2,1)} %all-gather.57.cloned.1.call-done, bf16[4096,1280]{0,1:T(8,128)(2,1)} %get-tuple-element.33, bf16[4096,5120]{1,0:T(8,128)(2,1)} %fusion.93.clone.2), kind=kOutput, calls=%fused_computation.121 | convolution fusion | flops 53718544384 | bytes 76038144 | tf_op jit(solution)/shard_map/dot_general | solution.py:21
  1017.7 66.9 %all-gather.33.cloned.1.call-done = bf16[1280,5120]{1,0:T(8,128)(2,1)} async-done(((bf16[640,5120]{1,0:T(8,128)(2,1)}), bf16[1280,5120]{1,0:T(8,128)(2,1)}) %all-gather.33.cloned.1.call-update) | async-done | bytes 13107216 | tf_op jit(solution)/shard_map/all_gather | solution.py:65
  1084.6 64.1 %convolution_convert_fusion.2 = bf16[4096,5120]{1,0:T(8,128)(2,1)} fusion(bf16[1280,5120]{1,0:T(8,128)(2,1)} %all-gather.33.cloned.1.call-done, bf16[4096,1280]{0,1:T(8,128)(2,1)} %get-tuple-element.35, f32[4096]{0:T(1024)S(1)} %add_rsqrt_fusion), kind=kOutput, calls=%fused_computation.83 | convolution fusion | flops 53723791360 | bytes 65552384 | tf_op jit(solution)/shard_map/dot_general | solution.py:28
  1148.8 93.6 %all-gather.31.cloned.1.call-done = bf16[5120,1280]{1,0:T(8,128)(2,1)} async-done(((bf16[2560,1280]{1,0:T(8,128)(2,1)}), bf16[5120,1280]{1,0:T(8,128)(2,1)}) %all-gather.31.cloned.1.call-update) | async-done | bytes 13107216 | tf_op jit(solution)/shard_map/all_gather | solution.py:66
  1242.4 115.6 %fusion.11 = bf16[4096,5120]{1,0:T(8,128)(2,1)} fusion(bf16[4096,5120]{1,0:T(8,128)(2,1)} %convolution_convert_fusion.2, bf16[4096,1280]{1,0:T(8,128)(2,1)} %param.5, bf16[5120,1280]{1,0:T(8,128)(2,1)} %all-gather.31.cloned.1.call-done), kind=kOutput, calls=%fused_computation.38 | convolution fusion | flops 54127493120 | bytes 107479040 | tf_op jit(solution)/shard_map/dot_general | solution.py:31
  1358.0 65.8 %fusion.69 = (f32[4096]{0:T(1024)S(1)}, f32[4096,1280]{0,1:T(8,128)}) fusion(bf16[4096,1280]{0,1:T(8,128)(2,1)} %get-tuple-element.35, f32[4096]{0:T(1024)S(1)} %copy-done.12, bf16[4096,5120]{1,0:T(8,128)(2,1)} %fusion.11, bf16[1280,5120]{1,0:T(8,128)(2,1)} %all-gather.33.cloned.1.call-done), kind=kOutput, calls=%fused_computation.102 | convolution fusion | flops 53708058624 | bytes 86540288 | tf_op jit(solution)/shard_map/dot_general | solution.py:35
  1423.8 16.5 fusion.73
  1440.3 0.5 all-gather.35.cloned.1.call-update
  1440.9 155.8 %all-gather.37.cloned.1.call-done = bf16[1280,5120]{1,0:T(8,128)(2,1)} async-done(((bf16[640,5120]{1,0:T(8,128)(2,1)}), bf16[1280,5120]{1,0:T(8,128)(2,1)}) %all-gather.37.cloned.1.call-update) | async-done | bytes 13107216 | tf_op jit(solution)/shard_map/all_gather | solution.py:65
  1596.7 64.1 %convolution_convert_fusion.1 = bf16[4096,5120]{1,0:T(8,128)(2,1)} fusion(bf16[1280,5120]{1,0:T(8,128)(2,1)} %all-gather.37.cloned.1.call-done, bf16[4096,1280]{0,1:T(8,128)(2,1)} %get-tuple-element.33, f32[4096]{0:T(1024)S(1)} %copy-done.8), kind=kOutput, calls=%fused_computation.82 | convolution fusion | flops 53723791360 | bytes 65552384 | tf_op jit(solution)/shard_map/dot_general | solution.py:28
  1660.8 93.7 %all-gather.35.cloned.1.call-done = bf16[5120,1280]{1,0:T(8,128)(2,1)} async-done(((bf16[2560,1280]{1,0:T(8,128)(2,1)}), bf16[5120,1280]{1,0:T(8,128)(2,1)}) %all-gather.35.cloned.1.call-update) | async-done | bytes 13107216 | tf_op jit(solution)/shard_map/all_gather | solution.py:66
  1754.5 121.1 %fusion.8 = bf16[4096,5120]{1,0:T(8,128)(2,1)} fusion(bf16[4096,5120]{1,0:T(8,128)(2,1)} %convolution_convert_fusion.1, bf16[4096,1280]{0,1:T(8,128)(2,1)} %fusion.73, bf16[5120,1280]{1,0:T(8,128)(2,1)} %all-gather.35.cloned.1.call-done), kind=kOutput, calls=%fused_computation.35 | convolution fusion | flops 54127493120 | bytes 107479040 | tf_op jit(solution)/shard_map/dot_general | solution.py:31
  1875.6 65.5 %fusion.74 = (f32[4096]{0:T(1024)S(1)}, f32[4096,1280]{0,1:T(8,128)}) fusion(bf16[4096,1280]{0,1:T(8,128)(2,1)} %get-tuple-element.33, f32[4096]{0:T(1024)S(1)} %copy-done.9, bf16[4096,5120]{1,0:T(8,128)(2,1)} %fusion.8, bf16[1280,5120]{1,0:T(8,128)(2,1)} %all-gather.37.cloned.1.call-done), kind=kOutput, calls=%fused_computation.107 | convolution fusion | flops 53708058624 | bytes 86540288 | tf_op jit(solution)/shard_map/dot_general | solution.py:35
  1941.1 16.4 fusion.78
  1957.6 0.5 all-gather.61.cloned.1.call-update
  1958.2 0.5 all-gather.39.cloned.1.call-update
  1958.8 0.5 all-gather.65.cloned.1.call-update
  1959.4 77.0 %fusion.52 = f32[5120,1280]{1,0:T(8,128)} fusion(bf16[4096,1280]{1,0:T(8,128)(2,1)} %param.5, bf16[4096,5120]{1,0:T(8,128)(2,1)} %convolution_convert_fusion.2), kind=kOutput, calls=%fused_computation.77 | convolution fusion | flops 53896806400 | bytes 78643200 | tf_op jit(solution)/shard_map/dot_general | solution.py:33
  2036.4 86.9 %fusion.50 = f32[5120,1280]{1,0:T(8,128)} fusion(bf16[4096,1280]{0,1:T(8,128)(2,1)} %fusion.73, bf16[4096,5120]{1,0:T(8,128)(2,1)} %convolution_convert_fusion.1), kind=kOutput, calls=%fused_computation.76 | convolution fusion | flops 53896806400 | bytes 78643200 | tf_op jit(solution)/shard_map/dot_general | solution.py:33
  2123.4 0.6 copy-done.4
  2124.0 64.1 %convolution_convert_fusion = bf16[4096,5120]{1,0:T(8,128)(2,1)} fusion(bf16[1280,5120]{1,0:T(8,128)(2,1)} %all-gather.41.cloned.1.call-done, bf16[4096,1280]{0,1:T(8,128)(2,1)} %copy.8, f32[4096]{0:T(1024)S(1)} %copy-done.4), kind=kOutput, calls=%fused_computation.81 | convolution fusion | flops 53723791360 | bytes 65552384 | tf_op jit(solution)/shard_map/dot_general | solution.py:28
  2188.1 87.0 %fusion.48 = f32[5120,1280]{1,0:T(8,128)} fusion(bf16[4096,1280]{0,1:T(8,128)(2,1)} %fusion.78, bf16[4096,5120]{1,0:T(8,128)(2,1)} %convolution_convert_fusion), kind=kOutput, calls=%fused_computation.75 | convolution fusion | flops 53896806400 | bytes 78643200 | tf_op jit(solution)/shard_map/dot_general | solution.py:33
  2275.2 0.6 copy-done.13
  2275.8 64.3 %fusion.117 = f32[1280,5120]{1,0:T(8,128)} fusion(bf16[4096,5120]{1,0:T(8,128)(2,1)} %fusion.11, bf16[4096,1280]{0,1:T(8,128)(2,1)} %get-tuple-element.35, f32[4096]{0:T(1024)S(1)} %copy-done.13), kind=kOutput, calls=%fused_computation.132 | convolution fusion | flops 53702819840 | bytes 78659584 | tf_op jit(solution)/shard_map/dot_general | solution.py:34
  2340.2 85.2 %fusion.218 = bf16[4096,5120]{1,0:T(8,128)(2,1)} fusion(bf16[1,1280,5120]{2,1,0:T(8,128)(2,1)} %all-gather.61.cloned.1.call-done, bf16[4096,1280]{0,1:T(8,128)(2,1)} %get-tuple-element.35, f32[4096]{0:T(1024)S(1)} %copy-done.13), kind=kOutput, calls=%fused_computation.56.clone.clone.clone.clone.1 | convolution fusion | flops 53933506560 | bytes 65552384 | tf_op jit(solution)/shard_map/dot_general | solution.py:19
  2425.4 64.2 %fusion.122 = f32[1280,5120]{1,0:T(8,128)} fusion(bf16[4096,5120]{1,0:T(8,128)(2,1)} %fusion.8, bf16[4096,1280]{0,1:T(8,128)(2,1)} %get-tuple-element.33, f32[4096]{0:T(1024)S(1)} %copy-done.10), kind=kOutput, calls=%fused_computation.133 | convolution fusion | flops 53702819840 | bytes 78659584 | tf_op jit(solution)/shard_map/dot_general | solution.py:34
  2489.7 121.4 %fusion.5 = bf16[4096,5120]{1,0:T(8,128)(2,1)} fusion(bf16[4096,5120]{1,0:T(8,128)(2,1)} %convolution_convert_fusion, bf16[4096,1280]{0,1:T(8,128)(2,1)} %fusion.78, bf16[5120,1280]{1,0:T(8,128)(2,1)} %all-gather.39.cloned.1.call-done), kind=kOutput, calls=%fused_computation.32 | convolution fusion | flops 54127493120 | bytes 107479040 | tf_op jit(solution)/shard_map/dot_general | solution.py:31
  2611.1 64.2 %fusion.127 = f32[1280,5120]{1,0:T(8,128)} fusion(bf16[4096,5120]{1,0:T(8,128)(2,1)} %fusion.5, bf16[4096,1280]{0,1:T(8,128)(2,1)} %copy.8, f32[4096]{0:T(1024)S(1)} %copy-done.5), kind=kOutput, calls=%fused_computation.134 | convolution fusion | flops 53702819840 | bytes 78659584 | tf_op jit(solution)/shard_map/dot_general | solution.py:34
  2675.4 90.5 %fusion.89 = bf16[4096,1280]{0,1:T(8,128)(2,1)} fusion(bf16[4096,1280]{0,1:T(8,128)(2,1)} %get-tuple-element.35, bf16[1,5120,1280]{2,1,0:T(8,128)(2,1)} %all-gather.65.cloned.1.call-done, bf16[4096,5120]{1,0:T(8,128)(2,1)} %fusion.218), kind=kOutput, calls=%fused_computation.122 | convolution fusion | flops 53702819840 | bytes 76021760 | tf_op jit(solution)/shard_map/dot_general | solution.py:21
  2765.9 15.0 copy.11
  2780.9 65.3 %fusion.79 = (f32[4096]{0:T(1024)S(1)}, f32[4096,1280]{0,1:T(8,128)}) fusion(bf16[4096,1280]{0,1:T(8,128)(2,1)} %copy.8, f32[4096]{0:T(1024)S(1)} %copy-done.6, bf16[4096,5120]{1,0:T(8,128)(2,1)} %fusion.5, bf16[1280,5120]{1,0:T(8,128)(2,1)} %all-gather.41.cloned.1.call-done), kind=kOutput, calls=%fused_computation.112 | convolution fusion | flops 53708058624 | bytes 86540288 | tf_op jit(solution)/shard_map/dot_general | solution.py:35
  2846.2 16.7 fusion.83
  2862.9 15.0 copy.12
  2878.0 18.6 reduce-scatter.15.cloned.1.call-done
  2896.6 154.8 %reduce-scatter.13.cloned.1.call-done = f32[640,1280]{1,0:T(8,128)} async-done(((f32[5120,1280]{1,0:T(8,128)}), f32[640,1280]{1,0:T(8,128)}) %reduce-scatter.13.cloned.1.call-update) | async-done | bytes 3276816 | tf_op jit(solution)/shard_map/reduce_scatter | solution.py:69
  3051.4 8.4 pad_maximum_fusion.1
  3059.8 146.4 %reduce-scatter.11.cloned.1.call-done = f32[160,5120]{1,0:T(8,128)} async-done(((f32[1280,5120]{1,0:T(8,128)}), f32[160,5120]{1,0:T(8,128)}) %reduce-scatter.11.cloned.1.call-update) | async-done | bytes 3276816 | tf_op jit(solution)/shard_map/reduce_scatter | solution.py:68
  3206.2 154.8 %reduce-scatter.9.cloned.1.call-done = f32[160,5120]{1,0:T(8,128)} async-done(((f32[1280,5120]{1,0:T(8,128)}), f32[160,5120]{1,0:T(8,128)}) %reduce-scatter.9.cloned.1.call-update) | async-done | bytes 3276816 | tf_op jit(solution)/shard_map/reduce_scatter | solution.py:68
  3361.0 154.6 %reduce-scatter.7.cloned.1.call-done = f32[160,5120]{1,0:T(8,128)} async-done(((f32[1280,5120]{1,0:T(8,128)}), f32[160,5120]{1,0:T(8,128)}) %reduce-scatter.7.cloned.1.call-update) | async-done | bytes 3276816 | tf_op jit(solution)/shard_map/reduce_scatter | solution.py:68
  3515.6 8.9 pad_maximum_fusion
  (75 shorter events, 1.3 us)
Async XLA Ops:
  7.2 53.0 %all-gather.43.cloned.1.call-start = ((), (), s32[]{:S(2)}) async-start(), calls=%async_computation.18 | async-start | bytes 8192000 | tf_op jit(solution)/shard_map/all_gather | solution.py:52
  12.0 95.4 %all-gather.47.cloned.1.call-start = ((), (), s32[]{:S(2)}) async-start(), calls=%async_computation.20 | async-start | bytes 8192000 | tf_op jit(solution)/shard_map/all_gather | solution.py:53
  16.9 137.2 %all-gather.51.cloned.1.call-start = ((), (), s32[]{:S(2)}) async-start(), calls=%async_computation.22 | async-start | bytes 8192000 | tf_op jit(solution)/shard_map/all_gather | solution.py:52
  17.6 183.6 %all-gather.55.cloned.1.call-start = ((), (), s32[]{:S(2)}) async-start(), calls=%async_computation.24 | async-start | bytes 8192000 | tf_op jit(solution)/shard_map/all_gather | solution.py:53
  18.2 230.1 %all-gather.59.cloned.1.call-start = ((), (), s32[]{:S(2)}) async-start(), calls=%async_computation.26 | async-start | bytes 8192000 | tf_op jit(solution)/shard_map/all_gather | solution.py:52
  18.8 276.7 %all-gather.63.cloned.1.call-start = ((), (), s32[]{:S(2)}) async-start(), calls=%async_computation.28 | async-start | bytes 8192000 | tf_op jit(solution)/shard_map/all_gather | solution.py:53
  19.3 434.0 %all-gather.45.cloned.1.call-start = ((), (), s32[]{:S(2)}) async-start(), calls=%async_computation.19 | async-start | bytes 19660800 | tf_op jit(solution)/shard_map/all_gather | solution.py:54
  60.2 551.0 %all-gather.49.cloned.1.call-start = ((), (), s32[]{:S(2)}) async-start(), calls=%async_computation.21 | async-start | bytes 19660800 | tf_op jit(solution)/shard_map/all_gather | solution.py:55
  107.4 661.6 %all-gather.53.cloned.1.call-start = ((), (), s32[]{:S(2)}) async-start(), calls=%async_computation.23 | async-start | bytes 19660800 | tf_op jit(solution)/shard_map/all_gather | solution.py:54
  154.1 772.7 %all-gather.57.cloned.1.call-start = ((), (), s32[]{:S(2)}) async-start(), calls=%async_computation.25 | async-start | bytes 19660800 | tf_op jit(solution)/shard_map/all_gather | solution.py:55
  201.2 883.4 %all-gather.33.cloned.1.call-start = ((), (), s32[]{:S(2)}) async-start(), calls=%async_computation.7 | async-start | bytes 19660800 | tf_op jit(solution)/shard_map/all_gather | solution.py:65
  295.4 946.9 %all-gather.31.cloned.1.call-start = ((), (), s32[]{:S(2)}) async-start(), calls=%async_computation.6 | async-start | bytes 19660800 | tf_op jit(solution)/shard_map/all_gather | solution.py:66
  315.9 222.4 %copy-start.3 = (f32[4096]{0:T(1024)}, f32[4096]{0:T(1024)S(1)}, u32[]{:S(2)}) copy-start(f32[4096]{0:T(1024)S(1)} %add_rsqrt_fusion.2) | copy-start | bytes 49156
  330.2 1266.5 %all-gather.37.cloned.1.call-start = ((), (), s32[]{:S(2)}) async-start(), calls=%async_computation.9 | async-start | bytes 19660800 | tf_op jit(solution)/shard_map/all_gather | solution.py:65
  701.8 152.2 %copy-start.7 = (f32[4096]{0:T(1024)}, f32[4096]{0:T(1024)S(1)}, u32[]{:S(2)}) copy-start(f32[4096]{0:T(1024)S(1)} %add_rsqrt_fusion.1) | copy-start | bytes 49156
  1017.7 131.1 %copy-start.11 = (f32[4096]{0:T(1024)}, f32[4096]{0:T(1024)S(1)}, u32[]{:S(2)}) copy-start(f32[4096]{0:T(1024)S(1)} %add_rsqrt_fusion) | copy-start | bytes 49156
  1242.4 115.6 %copy-start.12 = (f32[4096]{0:T(1024)S(1)}, f32[4096]{0:T(1024)}, u32[]{:S(2)}) copy-start(f32[4096]{0:T(1024)} %copy-done.11) | copy-start | bytes 49156
  1358.0 65.8 %copy-start.1 = (bf16[4096,1280]{0,1:T(8,128)(2,1)S(1)}, bf16[4096,1280]{0,1:T(8,128)(2,1)}, u32[]{:S(2)}) copy-start(bf16[4096,1280]{0,1:T(8,128)(2,1)} %copy.10) | copy-start | bytes 31457284
  1423.8 173.0 %copy-start.8 = (f32[4096]{0:T(1024)S(1)}, f32[4096]{0:T(1024)}, u32[]{:S(2)}) copy-start(f32[4096]{0:T(1024)} %copy-done.7) | copy-start | bytes 49156
  1440.3 314.2 %all-gather.35.cloned.1.call-start = ((), (), s32[]{:S(2)}) async-start(), calls=%async_computation.8 | async-start | bytes 19660800 | tf_op jit(solution)/shard_map/all_gather | solution.py:66
  1440.8 682.5 %all-gather.41.cloned.1.call-start = ((), (), s32[]{:S(2)}) async-start(), calls=%async_computation.11 | async-start | bytes 19660800 | tf_op jit(solution)/shard_map/all_gather | solution.py:65
  1754.5 121.1 %copy-start.9 = (f32[4096]{0:T(1024)S(1)}, f32[4096]{0:T(1024)}, u32[]{:S(2)}) copy-start(f32[4096]{0:T(1024)} %copy-done.7) | copy-start | bytes 49156
  1875.6 65.6 %copy-start.2 = (bf16[4096,1280]{0,1:T(8,128)(2,1)S(1)}, bf16[4096,1280]{0,1:T(8,128)(2,1)}, u32[]{:S(2)}) copy-start(bf16[4096,1280]{0,1:T(8,128)(2,1)} %fusion.73) | copy-start | bytes 31457284
  1957.6 382.6 %all-gather.61.cloned.1.call-start = ((), (), s32[]{:S(2)}) async-start(), calls=%async_computation.27 | async-start | bytes 19660800 | tf_op jit(solution)/shard_map/all_gather | solution.py:54
  1958.2 531.5 %all-gather.39.cloned.1.call-start = ((), (), s32[]{:S(2)}) async-start(), calls=%async_computation.10 | async-start | bytes 19660800 | tf_op jit(solution)/shard_map/all_gather | solution.py:66
  1958.7 716.6 %all-gather.65.cloned.1.call-start = ((), (), s32[]{:S(2)}) async-start(), calls=%async_computation.29 | async-start | bytes 19660800 | tf_op jit(solution)/shard_map/all_gather | solution.py:55
  1959.3 918.7 %reduce-scatter.17.cloned.1.call-start = ((), (), s32[]{:S(2)}) async-start(), calls=%async_computation.17 | async-start | bytes 29491200 | tf_op jit(solution)/shard_map/reduce_scatter | solution.py:69
  2036.4 860.2 %reduce-scatter.15.cloned.1.call-start = ((), (), s32[]{:S(2)}) async-start(), calls=%async_computation.16 | async-start | bytes 29491200 | tf_op jit(solution)/shard_map/reduce_scatter | solution.py:69
  2123.3 0.7 copy-start.4
  2123.3 928.1 %reduce-scatter.13.cloned.1.call-start = ((), (), s32[]{:S(2)}) async-start(), calls=%async_computation.15 | async-start | bytes 29491200 | tf_op jit(solution)/shard_map/reduce_scatter | solution.py:69
  2275.1 0.7 copy-start.13
  2275.1 931.0 %reduce-scatter.11.cloned.1.call-start = ((), (), s32[]{:S(2)}) async-start(), calls=%async_computation.14 | async-start | bytes 29491200 | tf_op jit(solution)/shard_map/reduce_scatter | solution.py:68
  2340.1 85.2 %copy-start.10 = (f32[4096]{0:T(1024)S(1)}, f32[4096]{0:T(1024)}, u32[]{:S(2)}) copy-start(f32[4096]{0:T(1024)} %copy-done.7) | copy-start | bytes 49156
  2340.1 1020.8 %reduce-scatter.9.cloned.1.call-start = ((), (), s32[]{:S(2)}) async-start(), calls=%async_computation.13 | async-start | bytes 29491200 | tf_op jit(solution)/shard_map/reduce_scatter | solution.py:68
  2489.6 1025.9 %reduce-scatter.7.cloned.1.call-start = ((), (), s32[]{:S(2)}) async-start(), calls=%async_computation.12 | async-start | bytes 29491200 | tf_op jit(solution)/shard_map/reduce_scatter | solution.py:68
  2489.7 121.4 %copy-start.5 = (f32[4096]{0:T(1024)S(1)}, f32[4096]{0:T(1024)}, u32[]{:S(2)}) copy-start(f32[4096]{0:T(1024)} %copy-done.3) | copy-start | bytes 49156
  2675.3 105.6 %copy-start.6 = (f32[4096]{0:T(1024)S(1)}, f32[4096]{0:T(1024)}, u32[]{:S(2)}) copy-start(f32[4096]{0:T(1024)} %copy-done.3) | copy-start | bytes 49156
  2780.9 65.3 %copy-start = (bf16[4096,1280]{0,1:T(8,128)(2,1)S(1)}, bf16[4096,1280]{0,1:T(8,128)(2,1)}, u32[]{:S(2)}) copy-start(bf16[4096,1280]{0,1:T(8,128)(2,1)} %copy.8) | copy-start | bytes 31457284
Sparse Core Ops, SparseCore 0:
  12.1 47.9 all-gather.42
  62.2 45.1 all-gather.46
  108.9 45.1 all-gather.50
  156.0 45.1 all-gather.54
  203.1 45.1 all-gather.58
  250.3 45.1 all-gather.62
  296.9 156.3 all-gather.44
  454.8 156.3 all-gather.48
  612.7 156.3 all-gather.52
  770.4 156.3 all-gather.56
  928.3 156.3 all-gather.32
  1086.0 156.3 all-gather.30
  1440.4 156.2 all-gather.36
  1598.1 156.3 all-gather.34
  1957.7 156.3 all-gather.40
  2115.4 156.3 all-gather.60
  2273.2 156.3 all-gather.38
  2430.9 156.3 all-gather.64
  2590.8 151.1 reduce-scatter.16
  2745.5 151.1 reduce-scatter.14
  2900.2 151.1 reduce-scatter.12
  3055.0 151.1 reduce-scatter.10
  3209.8 151.1 reduce-scatter.8
  3364.4 151.1 reduce-scatter.6
where the time goes:
time: 3540 us; the launch traced here: 3530 us
  matrix products  1720 us (49%)
  waiting for transfers between devices  1660 us (47%)
  other arithmetic  72.9 us (2%)
  local copies, waits for them, and re-layouts  69.6 us (2%)
    reduce_scatter x3, waiting for transfers between devices, device_step(): lax.psum_scatter(part_in, ('local', 'data'), scatter_dimension=0, tiled=T...  456 us
    all_gather x6, waiting for transfers between devices, device_step(): full_in = lax.all_gather(sub_in, 'local', axis=0, tiled=True)  413 us
    dot_general x3, matrix products, layer_backward(): lax.dot_general(grad_rows, w_out, LAST_LAST, preferred_element_type=jnp.f...  358 us
    all_gather x6, waiting for transfers between devices, device_step(): full_out = lax.all_gather(sub_out, 'local', axis=0, tiled=True)  333 us
    dot_general x3, matrix products, layer_forward(): branch = jnp.dot(hidden, w_out, preferred_element_type=jnp.float32)  272 us
    dot_general x3, matrix products, layer_forward(): jnp.dot(unit_rows, w_in, preferred_element_type=jnp.float32)  255 us
    dot_general x3, matrix products, layer_backward(): lax.dot_general(hidden, grad_rows, FIRST_FIRST, preferred_element_type=jn...  251 us
    dot_general x3, matrix products, layer_backward(): lax.dot_general(grad_pre, w_in, LAST_LAST, preferred_element_type=jnp.flo...  197 us
  transfers between devices with their start and end apart: 24, of which 19 were waited for; matrix products, arithmetic and copies ran while one was open for 41% of the time, Pallas kernels for 0%

commit v1 on v0

v1 whole, which is shorter than its diff:
```python
import functools

import jax
import jax.numpy as jnp
from jax import lax
from jax.experimental import pallas as pl
from jax.experimental.pallas import tpu as pltpu
from jax.sharding import Mesh, PartitionSpec as P


LAYERS = 3
D = 1280
F = 5120
T = 4096
NB = 4
NORM_EPS = 1e-6
C1 = 0.7978845608028654
C2 = C1 * 0.044715
LAST = (((1,), (1,)), ((), ()))
FIRST = (((0,), (0,)), ((), ()))
ANY = pl.BlockSpec(memory_space=pl.ANY)


def params(n):
    return pltpu.CompilerParams(vmem_limit_bytes=67000000, dimension_semantics=('arbitrary',) * n)


def norm_rows(x_wide):
    inv_rms = lax.rsqrt(jnp.mean(x_wide * x_wide, axis=-1, keepdims=True) + NORM_EPS)
    return x_wide * inv_rms, inv_rms


def gelu_fwd(a):
    t = jnp.tanh(a * (C1 + C2 * (a * a)))
    h = 0.5 * a
    return h + h * t


def gelu_both(a):
    a2 = a * a
    t = jnp.tanh(a * (C1 + C2 * a2))
    h = 0.5 * a
    slope = (0.5 + 0.5 * t) + (h * (1.0 - t * t)) * (C1 + (3.0 * C2) * a2)
    return h + h * t, slope


def load_weights(w1m, w1o, w2m, w2o, w1v, w2v, sems):
    c = lax.axis_index('c')
    r1 = D // 8
    r2 = F // 8
    copies = []
    for b in range(NB):
        for w1, w2, core in ((w1m, w2m, c), (w1o, w2o, 1 - c)):
            d = 2 * b + core
            copies.append(pltpu.make_async_copy(w1.at[pl.ds(b * r1, r1), :], w1v.at[pl.ds(pl.multiple_of(d * r1, r1), r1), :], sems.at[len(copies)]))
            copies.append(pltpu.make_async_copy(w2.at[pl.ds(b * r2, r2), :], w2v.at[pl.ds(pl.multiple_of(d * r2, r2), r2), :], sems.at[len(copies)]))
    for cp in copies:
        cp.start()
    for cp in copies:
        cp.wait()


WEIGHTS_VMEM = [pltpu.VMEM((D, F), jnp.bfloat16), pltpu.VMEM((F, D), jnp.bfloat16), pltpu.SemaphoreType.DMA((4 * NB,))]


def fwd_kernel(ch, x_ref, w1m, w1o, w2m, w2o, dep, o_ref, w1v, w2v, sems, u_s, acc):
    @pl.when(pl.program_id(0) == 0)
    def _():
        load_weights(w1m, w1o, w2m, w2o, w1v, w2v, sems)

    x_wide = x_ref[...].astype(jnp.float32)
    u_s[...] = norm_rows(x_wide)[0].astype(jnp.bfloat16)
    acc[...] = x_wide
    for j in range(F // ch):
        cols = pl.ds(j * ch, ch)
        a = jnp.dot(u_s[...], w1v[:, cols], preferred_element_type=jnp.float32).astype(jnp.bfloat16).astype(jnp.float32)
        s = gelu_fwd(a).astype(jnp.bfloat16)
        acc[...] += jnp.dot(s, w2v[cols, :], preferred_element_type=jnp.float32)
    o_ref[...] = acc[...].astype(jnp.bfloat16)


def fwd_call(x, w1m, w1o, w2m, w2o, dep, tm=512, ch=1024):
    row = pl.BlockSpec((tm, D), lambda i: (i, 0))
    return pl.pallas_call(
        functools.partial(fwd_kernel, ch), grid=(T // tm,), in_specs=[row] + [ANY] * 5, out_specs=row,
        out_shape=jax.ShapeDtypeStruct((T, D), jnp.bfloat16),
        scratch_shapes=WEIGHTS_VMEM + [pltpu.VMEM((tm, D), jnp.bfloat16), pltpu.VMEM((tm, D), jnp.float32)],
        compiler_params=params(1),
        cost_estimate=pl.CostEstimate(flops=4 * T * D * F, bytes_accessed=50000000, transcendentals=T * F),
        name='mlp_fwd')(x, w1m, w1o, w2m, w2o, dep)


def bwd_kernel(sub, full, x_ref, dy_ref, w1m, w1o, w2m, w2o, dep, s_ref, da_ref, ut_ref, *refs):
    w1v, w2v, sems, u_s = refs[-4:]
    i = pl.program_id(0)
    j = pl.program_id(1)

    @pl.when((i == 0) & (j == 0))
    def _():
        load_weights(w1m, w1o, w2m, w2o, w1v, w2v, sems)

    @pl.when(j == 0)
    def _():
        u = norm_rows(x_ref[...].astype(jnp.float32))[0].astype(jnp.bfloat16)
        u_s[...] = u
        ut_ref[...] = u.T

    ch = s_ref.shape[1]
    for k in range(ch // sub):
        cols = pl.ds(pl.multiple_of(j * ch + k * sub, sub), sub)
        a = jnp.dot(u_s[...], w1v[:, cols], preferred_element_type=jnp.float32).astype(jnp.bfloat16).astype(jnp.float32)
        ds = lax.dot_general(dy_ref[...], w2v[cols, :], LAST, preferred_element_type=jnp.float32)
        s, slope = gelu_both(a)
        s_ref[:, k * sub:(k + 1) * sub] = s.astype(jnp.bfloat16)
        da_ref[:, k * sub:(k + 1) * sub] = (slope * ds).astype(jnp.bfloat16)
    if not full:
        return
    dx_ref, acc = refs[:2]
    cols = pl.ds(pl.multiple_of(j * ch, ch), ch)
    du = lax.dot_general(da_ref[...], w1v[:, cols], LAST, preferred_element_type=jnp.float32)

    @pl.when(j == 0)
    def _():
        acc[...] = du

    @pl.when(j > 0)
    def _():
        acc[...] += du

    @pl.when(j == pl.num_programs(1) - 1)
    def _():
        dx_ref[...] = norm_back(x_ref[...], dy_ref[...], acc[...])


def norm_back(x, dy, du):
    v, inv_rms = norm_rows(x.astype(jnp.float32))
    m = jnp.mean(du * v, axis=-1, keepdims=True)
    return (dy.astype(jnp.float32) + inv_rms * (du - v * m)).astype(jnp.bfloat16)


def bwd_call(x, dy, w1m, w1o, w2m, w2o, dep, full=True, tm=512, ch=2560, sub=512):
    row = pl.BlockSpec((tm, D), lambda i, j: (i, 0))
    hid = pl.BlockSpec((tm, ch), lambda i, j: (i, j))
    n = int(full)
    return pl.pallas_call(
        functools.partial(bwd_kernel, sub, full), grid=(T // tm, F // ch), in_specs=[row, row] + [ANY] * 5,
        out_specs=[hid, hid, pl.BlockSpec((D, tm), lambda i, j: (0, i))] + [row] * n,
        out_shape=[jax.ShapeDtypeStruct((T, F), jnp.bfloat16)] * 2 + [jax.ShapeDtypeStruct((D, T), jnp.bfloat16)] + [jax.ShapeDtypeStruct((T, D), jnp.bfloat16)] * n,
        scratch_shapes=[pltpu.VMEM((tm, D), jnp.float32)] * n + WEIGHTS_VMEM + [pltpu.VMEM((tm, D), jnp.bfloat16)],
        compiler_params=params(2),
        cost_estimate=pl.CostEstimate(flops=(4 + 2 * n) * T * D * F, bytes_accessed=150000000, transcendentals=T * F),
        name='mlp_bwd')(x, dy, w1m, w1o, w2m, w2o, dep)


def du_kernel(x_ref, dy_ref, da_ref, w1m, w1o, dep, dx_ref, w1v, sems):
    @pl.when(pl.program_id(0) == 0)
    def _():
        c = lax.axis_index('c')
        r = D // 8
        copies = []
        for b in range(NB):
            for w1, core in ((w1m, c), (w1o, 1 - c)):
                d = 2 * b + core
                copies.append(pltpu.make_async_copy(w1.at[pl.ds(b * r, r), :], w1v.at[pl.ds(pl.multiple_of(d * r, r), r), :], sems.at[len(copies)]))
        for cp in copies:
            cp.start()
        for cp in copies:
            cp.wait()

    du = lax.dot_general(da_ref[...], w1v[...], LAST, preferred_element_type=jnp.float32)
    dx_ref[...] = norm_back(x_ref[...], dy_ref[...], du)


def du_call(x, dy, da, w1m, w1o, dep, tm=512):
    row = pl.BlockSpec((tm, D), lambda i: (i, 0))
    return pl.pallas_call(
        du_kernel, grid=(T // tm,), in_specs=[row, row, pl.BlockSpec((tm, F), lambda i: (i, 0))] + [ANY] * 3, out_specs=row,
        out_shape=jax.ShapeDtypeStruct((T, D), jnp.bfloat16),
        scratch_shapes=[pltpu.VMEM((D, F), jnp.bfloat16), pltpu.SemaphoreType.DMA((2 * NB,))],
        compiler_params=params(1),
        cost_estimate=pl.CostEstimate(flops=2 * T * D * F, bytes_accessed=80000000, transcendentals=0),
        name='grad_x')(x, dy, da, w1m, w1o, dep)


def wout_kernel(cs, s_ref, dy_ref, dep, *refs):
    v = lax.dot_general(s_ref[...], dy_ref[...], FIRST, preferred_element_type=jnp.float32)
    refs[-1][...] = v + refs[0][...] if len(refs) == 2 else v


def wout_call(s, dy, core, dep, recv=None):
    extra = [] if recv is None else [recv]
    bm = F // 8
    blk = pl.BlockSpec((bm, D), lambda b, cs: (b, 0))
    spec = pltpu.PrefetchScalarGridSpec(
        num_scalar_prefetch=1, grid=(NB,),
        in_specs=[pl.BlockSpec((T, bm), lambda b, cs: (0, 2 * b + cs[0])), pl.BlockSpec((T, D), lambda b, cs: (0, 0), pipeline_mode=pl.Buffered(1)), ANY] + [blk] * len(extra),
        out_specs=blk)
    return pl.pallas_call(
        wout_kernel, grid_spec=spec, out_shape=jax.ShapeDtypeStruct((F // 2, D), jnp.float32), compiler_params=params(1),
        cost_estimate=pl.CostEstimate(flops=T * D * F, bytes_accessed=50000000, transcendentals=0),
        name='grad_w_out')(core, s, dy, dep, *extra)


def win_kernel(cs, ut, da_ref, dep, *refs):
    o_ref, lhs, sems = refs[-3:]

    @pl.when(pl.program_id(0) == 0)
    def _():
        r = D // 8
        copies = [pltpu.make_async_copy(ut.at[pl.ds(pl.multiple_of((2 * b + cs[0]) * r, r), r), :], lhs.at[pl.ds(b * r, r), :], sems.at[b]) for b in range(NB)]
        for cp in copies:
            cp.start()
        for cp in copies:
            cp.wait()

    v = jnp.dot(lhs[...], da_ref[...], preferred_element_type=jnp.float32)
    o_ref[...] = v + refs[0][...] if len(refs) == 4 else v


def win_call(ut, da, core, dep, recv=None, bn=512):
    extra = [] if recv is None else [recv]
    blk = pl.BlockSpec((D // 2, bn), lambda n, cs: (0, n))
    spec = pltpu.PrefetchScalarGridSpec(
        num_scalar_prefetch=1, grid=(F // bn,),
        in_specs=[ANY, pl.BlockSpec((T, bn), lambda n, cs: (0, n)), ANY] + [blk] * len(extra), out_specs=blk,
        scratch_shapes=[pltpu.VMEM((D // 2, T), jnp.bfloat16), pltpu.SemaphoreType.DMA((NB,))])
    return pl.pallas_call(
        win_kernel, grid_spec=spec, out_shape=jax.ShapeDtypeStruct((D // 2, F), jnp.float32), compiler_params=params(1),
        cost_estimate=pl.CostEstimate(flops=T * D * F, bytes_accessed=50000000, transcendentals=0),
        name='grad_w_in')(core, ut, da, dep, *extra)


SWAP = [(0, 1), (1, 0)]
CHIPS = ('y', 'x')
ALL = ('y', 'x', 'c')


def swap(v):
    return lax.ppermute(v, 'c', SWAP)


def place(stack, item, l):
    return lax.dynamic_update_slice(stack, item[None], (l, 0, 0))


def solution(mesh):
    fine = Mesh(mesh.devices.reshape(2, 2, 2), ALL)

    def device_step(x_rows, grad_rows, w_in, w_out):
        me = lax.axis_index('c').astype(jnp.int32)[None]
        other = 1 - me

        def gather(l, tok):
            p1, p2 = w_in[l], w_out[l]
            if tok:
                p1, p2 = lax.optimization_barrier((p1, p2) + tok)[:2]
            g1 = lax.all_gather(p1, CHIPS, axis=0, tiled=True)
            g2 = lax.all_gather(p2, CHIPS, axis=0, tiled=True)
            return g1, g2

        kept = [gather(0, ())]
        xs = [x_rows]
        for l in range(LAYERS - 1):
            kept.append(gather(l + 1, kept[-1]))
            w1, w2 = kept[l]
            w1o, w2o = swap(w1), swap(w2)
            xs.append(fwd_call(xs[-1], w1, w1o, w2, w2o, x_rows))
        grad = grad_rows
        tok = xs[-1]
        out_in = jnp.zeros((LAYERS, D // 8, F), jnp.float32)
        out_out = jnp.zeros((LAYERS, F // 8, D), jnp.float32)
        for l in reversed(range(LAYERS)):
            w1, w2 = kept[l]
            if l < LAYERS - 1:
                w1, w2 = lax.optimization_barrier((w1, w2, grad))[:2]
            w1o = swap(w1)
            s, da, ut, *rest = bwd_call(xs[l], grad, w1, w1o, w2, swap(w2), tok, full=l > 0)
            send_out = wout_call(s, grad, other, tok)
            send_in = win_call(ut, da, other, send_out)
            recv_in = swap(send_in)
            part_out = wout_call(s, grad, me, send_in, swap(send_out))
            out_out = place(out_out, lax.psum_scatter(part_out, CHIPS, scatter_dimension=0, tiled=True), l)
            part_in = win_call(ut, da, me, part_out, recv_in)
            out_in = place(out_in, lax.psum_scatter(part_in, CHIPS, scatter_dimension=0, tiled=True), l)
            tok = part_in
            grad = rest[0] if rest else du_call(xs[l], grad, da, w1, w1o, tok)
        w1, w2 = lax.optimization_barrier(kept[-1] + (send_in,))[:2]
        x_out = fwd_call(xs[-1], w1, swap(w1), w2, swap(w2), tok)
        return x_out, out_in, out_out, grad

    row = P(ALL, None)
    wt = P(None, ALL, None)
    return jax.shard_map(device_step, mesh=fine, in_specs=(row, row, wt, wt), out_specs=(row, wt, wt, row), check_vma=False)
```

time: 3540 us -> 1900 us (0.54)
  matrix products: 1720 us -> 0 us
  Pallas kernels: 0 us -> 1490 us
  waiting for transfers between devices: 1660 us -> 349 us
  other arithmetic: 72.9 us -> 0 us
    dot_general x21 -> x0, matrix products: 1720 us -> none  [the longest x3 358 us: layer_backward(): lax.dot_general(grad_rows, w_out, LAST_LAST, preferred_element_type=jnp.f...]
    pallas_call x0 -> x19, Pallas kernels: none -> 1490 us  [the longest x3 589 us: bwd_call(): pl.pallas_call(functools.partial(bwd_kernel, sub, full), grid=(T // tm, F...]
    all_gather x18 -> x6, waiting for transfers between devices: 1020 us -> 270 us  [the longest x3 137 us: gather(): g2 = lax.all_gather(p2, CHIPS, axis=0, tiled=True)]
    reduce_scatter x6, waiting for transfers between devices: 629 us -> 0.03 us  [the longest x3 0.02 us: device_step(): lax.psum_scatter(part_out, CHIPS, scatter_dimension=0, tiled=True)]
    ppermute x0 -> x18, waiting for transfers between devices: none -> 77.9 us  [swap(): return lax.ppermute(v, 'c', SWAP)]
    convert_element_type x3 -> x0, other arithmetic: 49.6 us -> none  [layer_backward(): return (grad_x.astype(jnp.bfloat16), grad_w_in, grad_w_out)]
    unnamed x31 -> x0, local copies, waits for them, and re-layouts: 45.7 us -> none
  transfers between devices with their start and end apart: 24 -> 30, of which waited for: 19 -> 9; matrix products, arithmetic and copies ran while one was open for 41% -> 2% of each run, Pallas kernels for 0% -> 63%
where the time goes in v1:
time: 1900 us; the launch traced here: 1890 us
  Pallas kernels  1490 us (78%)
  waiting for transfers between devices  349 us (18%)
  local copies, waits for them, and re-layouts  38.8 us (2%)
    pallas_call x3, Pallas kernels, bwd_call(): pl.pallas_call(functools.partial(bwd_kernel, sub, full), grid=(T // tm, F...  589 us
    pallas_call x3, Pallas kernels, fwd_call(): pl.pallas_call(functools.partial(fwd_kernel, ch), grid=(T // tm,), in_spe...  388 us
    pallas_call x6, Pallas kernels, win_call(): pl.pallas_call(win_kernel, grid_spec=spec, out_shape=jax.ShapeDtypeStruct...  221 us
    pallas_call x6, Pallas kernels, wout_call(): pl.pallas_call(wout_kernel, grid_spec=spec, out_shape=jax.ShapeDtypeStruc...  216 us
    all_gather x3, waiting for transfers between devices, gather(): g2 = lax.all_gather(p2, CHIPS, axis=0, tiled=True)  137 us
    all_gather x3, waiting for transfers between devices, gather(): g1 = lax.all_gather(p1, CHIPS, axis=0, tiled=True)  133 us
    ppermute x18, waiting for transfers between devices, swap(): return lax.ppermute(v, 'c', SWAP)  77.9 us
    pallas_call x1, Pallas kernels, du_call(): pl.pallas_call(du_kernel, grid=(T // tm,), in_specs=[row, row, pl.BlockSp...  72.9 us
  transfers between devices with their start and end apart: 30, of which 9 were waited for; matrix products, arithmetic and copies ran while one was open for 2% of the time, Pallas kernels for 63%

profile of v1, /device:TPU:0, one launch (start us, length us, event | category | flops | bytes accessed | tf_op | source)
XLA Modules:
  0.0 1893.6 jit_solution(14278423646124044540)
XLA Ops:
  7.2 0.0 all-gather.17.cloned.1.call-start
  7.2 4.8 slice_bitcast_fusion.1
  12.0 0.0 all-gather.19.cloned.1.call-start
  12.1 4.8 slice_bitcast_fusion
  16.9 0.0 all-gather.9.cloned.1.call-start
  16.9 64.7 %all-gather.17.cloned.1.call-done = bf16[1,640,5120]{2,1,0:T(8,128)(2,1)} async-done(((bf16[1,160,5120]{2,1,0:T(8,128)(2,1)}), bf16[1,640,5120]{2,1,0:T(8,128)(2,1)}) %all-gather.17.cloned.1.call-update) | async-done | bytes 6553616 | tf_op jit(solution)/shard_map/all_gather | solution.py:257
  81.6 68.5 %all-gather.19.cloned.1.call-done = bf16[1,2560,1280]{2,1,0:T(8,128)(2,1)} async-done(((bf16[1,640,1280]{2,1,0:T(8,128)(2,1)}), bf16[1,2560,1280]{2,1,0:T(8,128)(2,1)}) %all-gather.19.cloned.1.call-update) | async-done | bytes 6553616 | tf_op jit(solution)/shard_map/all_gather | solution.py:258
  150.1 0.0 all-gather.11.cloned.1.call-start
  150.1 0.5 all-gather.11.cloned.1.call-update
  150.7 68.4 %all-gather.9.cloned.1.call-done.w1m = bf16[640,5120]{1,0:T(8,128)(2,1)} async-done(((bf16[160,5120]{1,0:T(8,128)(2,1)}), bf16[640,5120]{1,0:T(8,128)(2,1)}) %all-gather.9.cloned.1.call-update) | async-done | bytes 6553616 | tf_op jit(solution)/shard_map/all_gather | solution.py:257
  219.1 68.3 %all-gather.11.cloned.1.call-done.w2m = bf16[2560,1280]{1,0:T(8,128)(2,1)} async-done(((bf16[640,1280]{1,0:T(8,128)(2,1)}), bf16[2560,1280]{1,0:T(8,128)(2,1)}) %all-gather.11.cloned.1.call-update) | async-done | bytes 6553616 | tf_op jit(solution)/shard_map/all_gather | solution.py:258
  287.4 0.0 all-gather.15.cloned.1.call-start
  287.5 0.5 collective-permute-start.1
  288.0 0.0 reduce-scatter.13.cloned.1.call-start
  288.1 0.1 collective-permute-start.2
  288.1 0.5 collective-permute-start.3
  288.6 9.8 collective-permute-done.w1o
  298.4 9.4 collective-permute-done.1.w2o
  307.7 128.8 %mlp_fwd.3.x_ref = bf16[4096,1280]{1,0:T(8,128)(2,1)} custom-call(bf16[4096,1280]{1,0:T(8,128)(2,1)} %x_ref.5, bf16[640,5120]{1,0:T(8,128)(2,1)} %bitcast.24, bf16[640,5120]{1,0:T(8,128)(2,1)} %collective-permute-done.w1o, bf16[2560,1280]{1,0:T(8,128)(2,1)} %bitcast.29, bf16[2560,1280]{1,0:T(8,128)(2,1)} %collective-permute-done.1.w2o, bf16[4096,1280]{1,0:T(8,128)(2,1)} %x_ref.5), custom_call_target="tpu_custom_call" | custom-call | flops 107374182400 | bytes 50000000 | tf_op jit(solution)/shard_map/mlp_fwd/pallas_call | solution.py:84
  436.6 0.1 collective-permute-start.4
  436.8 0.4 collective-permute-start.5
  437.1 129.4 %mlp_fwd.4.x_ref.dep = bf16[4096,1280]{1,0:T(8,128)(2,1)} custom-call(bf16[4096,1280]{1,0:T(8,128)(2,1)} %mlp_fwd.3.x_ref, bf16[640,5120]{1,0:T(8,128)(2,1)} %all-gather.9.cloned.1.call-done.w1m, bf16[640,5120]{1,0:T(8,128)(2,1)} %collective-permute-done.2.w1o, bf16[2560,1280]{1,0:T(8,128)(2,1)} %all-gather.11.cloned.1.call-done.w2m, ...), custom_call_target="tpu_custom_call" | custom-call | flops 107374182400 | bytes 50000000 | tf_op jit(solution)/shard_map/mlp_fwd/pallas_call | solution.py:84
  566.5 218.4 %mlp_bwd.3 = (bf16[4096,5120]{1,0:T(8,128)(2,1)}, bf16[4096,5120]{1,0:T(8,128)(2,1)}, bf16[1280,4096]{1,0:T(8,128)(2,1)}, bf16[4096,1280]{1,0:T(8,128)(2,1)}) custom-call(bf16[4096,1280]{1,0:T(8,128)(2,1)} %mlp_fwd.4.x_ref.dep, bf16[4096,1280]{1,0:T(8,128)(2,1)} %dy_ref.5, bf16[640,5120]{1,0:T(8,128)(2,1)} %all-gather.13.cloned.1.call-done.w1m, ...), custom_call_target="tpu_custom_call" | custom-call | flops 161061273600 | bytes 150000000 | tf_op jit(solution)/shard_map/mlp_bwd/pallas_call | solution.py:145
  784.9 35.6 %grad_w_out.6.dep = f32[2560,1280]{1,0:T(8,128)} custom-call(s32[1]{0:T(128)S(6)} %sub.3.cs, bf16[4096,5120]{1,0:T(8,128)(2,1)} %get-tuple-element.34.s_ref, bf16[4096,1280]{1,0:T(8,128)(2,1)} %dy_ref.5, bf16[4096,1280]{1,0:T(8,128)(2,1)} %mlp_fwd.4.x_ref.dep), custom_call_target="tpu_custom_call" | custom-call | flops 26843545600 | bytes 50000000 | tf_op jit(solution)/shard_map/grad_w_out/pallas_call | solution.py:198
  820.5 0.2 collective-permute-start.8
  820.7 35.2 %grad_w_in.6.dep = f32[640,5120]{1,0:T(8,128)} custom-call(s32[1]{0:T(128)S(6)} %sub.3.cs, bf16[1280,4096]{1,0:T(8,128)(2,1)} %get-tuple-element.32.ut, bf16[4096,5120]{1,0:T(8,128)(2,1)} %get-tuple-element.33.da_ref, f32[2560,1280]{1,0:T(8,128)} %grad_w_out.6.dep), custom_call_target="tpu_custom_call" | custom-call | flops 26843545600 | bytes 50000000 | tf_op jit(solution)/shard_map/grad_w_in/pallas_call | solution.py:227
  856.0 36.4 %grad_w_out.7.dep = f32[2560,1280]{1,0:T(8,128)} custom-call(s32[1]{0:T(128)} %bitcast.6.cs, bf16[4096,5120]{1,0:T(8,128)(2,1)} %get-tuple-element.34.s_ref, bf16[4096,1280]{1,0:T(8,128)(2,1)} %dy_ref.5, f32[640,5120]{1,0:T(8,128)} %grad_w_in.6.dep, f32[2560,1280]{1,0:T(8,128)} %collective-permute-done.8.refs_0_), custom_call_target="tpu_custom_call" | custom-call | flops 26843545600 | bytes 50000000 | tf_op jit(solution)/shard_map/grad_w_out/pallas_call | solution.py:198
  892.3 0.0 reduce-scatter.7.cloned.1.call-start
  892.4 0.3 collective-permute-start.9
  892.7 0.2 collective-permute-start.6
  892.9 0.3 collective-permute-start.7
  893.2 19.4 %collective-permute-done.9.refs_0_ = f32[640,5120]{1,0:T(8,128)} collective-permute-done((f32[640,5120]{1,0:T(8,128)}, f32[640,5120]{1,0:T(8,128)}, u32[]{:S(2)}, u32[]{:S(2)}) %collective-permute-start.9) | collective-permute-done | bytes 13107232 | tf_op jit(solution)/shard_map/ppermute | solution.py:239
  912.7 38.3 %grad_w_in.7.dep = f32[640,5120]{1,0:T(8,128)} custom-call(s32[1]{0:T(128)} %bitcast.6.cs, bf16[1280,4096]{1,0:T(8,128)(2,1)} %get-tuple-element.32.ut, bf16[4096,5120]{1,0:T(8,128)(2,1)} %get-tuple-element.33.da_ref, f32[2560,1280]{1,0:T(8,128)} %grad_w_out.7.dep, f32[640,5120]{1,0:T(8,128)} %collective-permute-done.9.refs_0_), custom_call_target="tpu_custom_call" | custom-call | flops 26843545600 | bytes 50000000 | tf_op jit(solution)/shard_map/grad_w_in/pallas_call | solution.py:227
  951.0 0.0 reduce-scatter.15.cloned.1.call-start
  951.1 219.1 %mlp_bwd.4 = (bf16[4096,5120]{1,0:T(8,128)(2,1)}, bf16[4096,5120]{1,0:T(8,128)(2,1)}, bf16[1280,4096]{1,0:T(8,128)(2,1)}, bf16[4096,1280]{1,0:T(8,128)(2,1)}) custom-call(bf16[4096,1280]{1,0:T(8,128)(2,1)} %mlp_fwd.3.x_ref, bf16[4096,1280]{1,0:T(8,128)(2,1)} %get-tuple-element.29.dy_ref, bf16[640,5120]{1,0:T(8,128)(2,1)} %all-gather.9.cloned.1.call-done.w1m, ...), custom_call_target="tpu_custom_call" | custom-call | flops 161061273600 | bytes 150000000 | tf_op jit(solution)/shard_map/mlp_bwd/pallas_call | solution.py:145
  1170.2 35.4 %grad_w_out.8.dep = f32[2560,1280]{1,0:T(8,128)} custom-call(s32[1]{0:T(128)S(6)} %sub.3.cs, bf16[4096,5120]{1,0:T(8,128)(2,1)} %get-tuple-element.40.s_ref, bf16[4096,1280]{1,0:T(8,128)(2,1)} %get-tuple-element.29.dy_ref, f32[640,5120]{1,0:T(8,128)} %grad_w_in.7.dep), custom_call_target="tpu_custom_call" | custom-call | flops 26843545600 | bytes 50000000 | tf_op jit(solution)/shard_map/grad_w_out/pallas_call | solution.py:198
  1205.6 0.2 collective-permute-start.12
  1205.8 35.2 %grad_w_in.8.dep = f32[640,5120]{1,0:T(8,128)} custom-call(s32[1]{0:T(128)S(6)} %sub.3.cs, bf16[1280,4096]{1,0:T(8,128)(2,1)} %get-tuple-element.38.ut, bf16[4096,5120]{1,0:T(8,128)(2,1)} %get-tuple-element.39.da_ref, f32[2560,1280]{1,0:T(8,128)} %grad_w_out.8.dep), custom_call_target="tpu_custom_call" | custom-call | flops 26843545600 | bytes 50000000 | tf_op jit(solution)/shard_map/grad_w_in/pallas_call | solution.py:227
  1241.0 36.3 %grad_w_out.9.dep = f32[2560,1280]{1,0:T(8,128)} custom-call(s32[1]{0:T(128)} %bitcast.6.cs, bf16[4096,5120]{1,0:T(8,128)(2,1)} %get-tuple-element.40.s_ref, bf16[4096,1280]{1,0:T(8,128)(2,1)} %get-tuple-element.29.dy_ref, f32[640,5120]{1,0:T(8,128)} %grad_w_in.8.dep, f32[2560,1280]{1,0:T(8,128)} %collective-permute-done.12.refs_0_), custom_call_target="tpu_custom_call" | custom-call | flops 26843545600 | bytes 50000000 | tf_op jit(solution)/shard_map/grad_w_out/pallas_call | solution.py:198
  1277.3 0.0 reduce-scatter.9.cloned.1.call-start
  1277.4 0.3 collective-permute-start.13
  1277.7 0.2 collective-permute-start.10
  1277.9 0.3 collective-permute-start.11
  1278.2 19.4 %collective-permute-done.13.refs_0_ = f32[640,5120]{1,0:T(8,128)} collective-permute-done((f32[640,5120]{1,0:T(8,128)}, f32[640,5120]{1,0:T(8,128)}, u32[]{:S(2)}, u32[]{:S(2)}) %collective-permute-start.13) | collective-permute-done | bytes 13107232 | tf_op jit(solution)/shard_map/ppermute | solution.py:239
  1297.6 38.2 %grad_w_in.9.dep = f32[640,5120]{1,0:T(8,128)} custom-call(s32[1]{0:T(128)} %bitcast.6.cs, bf16[1280,4096]{1,0:T(8,128)(2,1)} %get-tuple-element.38.ut, bf16[4096,5120]{1,0:T(8,128)(2,1)} %get-tuple-element.39.da_ref, f32[2560,1280]{1,0:T(8,128)} %grad_w_out.9.dep, f32[640,5120]{1,0:T(8,128)} %collective-permute-done.13.refs_0_), custom_call_target="tpu_custom_call" | custom-call | flops 26843545600 | bytes 50000000 | tf_op jit(solution)/shard_map/grad_w_in/pallas_call | solution.py:227
  1335.9 0.0 reduce-scatter.17.cloned.1.call-start
  1336.0 151.7 %mlp_bwd.5 = (bf16[4096,5120]{1,0:T(8,128)(2,1)}, bf16[4096,5120]{1,0:T(8,128)(2,1)}, bf16[1280,4096]{1,0:T(8,128)(2,1)}) custom-call(bf16[4096,1280]{1,0:T(8,128)(2,1)} %x_ref.5, bf16[4096,1280]{1,0:T(8,128)(2,1)} %get-tuple-element.35.dy_ref, bf16[640,5120]{1,0:T(8,128)(2,1)} %bitcast.26, bf16[640,5120]{1,0:T(8,128)(2,1)} %collective-permute-done.10.w1o, ...), custom_call_target="tpu_custom_call" | custom-call | flops 107374182400 | bytes 150000000 | tf_op jit(solution)/shard_map/mlp_bwd/pallas_call | solution.py:145
  1487.7 35.9 %grad_w_out.10.dep = f32[2560,1280]{1,0:T(8,128)} custom-call(s32[1]{0:T(128)S(6)} %sub.3.cs, bf16[4096,5120]{1,0:T(8,128)(2,1)} %get-tuple-element.43.s_ref, bf16[4096,1280]{1,0:T(8,128)(2,1)} %get-tuple-element.35.dy_ref, f32[640,5120]{1,0:T(8,128)} %grad_w_in.9.dep), custom_call_target="tpu_custom_call" | custom-call | flops 26843545600 | bytes 50000000 | tf_op jit(solution)/shard_map/grad_w_out/pallas_call | solution.py:198
  1523.6 35.3 %grad_w_in.10.dep = f32[640,5120]{1,0:T(8,128)} custom-call(s32[1]{0:T(128)S(6)} %sub.3.cs, bf16[1280,4096]{1,0:T(8,128)(2,1)} %get-tuple-element.41.ut, bf16[4096,5120]{1,0:T(8,128)(2,1)} %get-tuple-element.42.da_ref, f32[2560,1280]{1,0:T(8,128)} %grad_w_out.10.dep), custom_call_target="tpu_custom_call" | custom-call | flops 26843545600 | bytes 50000000 | tf_op jit(solution)/shard_map/grad_w_in/pallas_call | solution.py:227
  1559.0 36.2 %grad_w_out.11.dep = f32[2560,1280]{1,0:T(8,128)} custom-call(s32[1]{0:T(128)} %bitcast.6.cs, bf16[4096,5120]{1,0:T(8,128)(2,1)} %get-tuple-element.43.s_ref, bf16[4096,1280]{1,0:T(8,128)(2,1)} %get-tuple-element.35.dy_ref, f32[640,5120]{1,0:T(8,128)} %grad_w_in.10.dep, f32[2560,1280]{1,0:T(8,128)} %collective-permute-done.16.refs_0_), custom_call_target="tpu_custom_call" | custom-call | flops 26843545600 | bytes 50000000 | tf_op jit(solution)/shard_map/grad_w_out/pallas_call | solution.py:198
  1595.2 0.0 reduce-scatter.11.cloned.1.call-start
  1595.3 0.5 collective-permute-start.17
  1595.7 19.9 %collective-permute-done.17.refs_0_ = f32[640,5120]{1,0:T(8,128)} collective-permute-done((f32[640,5120]{1,0:T(8,128)}, f32[640,5120]{1,0:T(8,128)}, u32[]{:S(2)}, u32[]{:S(2)}) %collective-permute-start.17) | collective-permute-done | bytes 13107232 | tf_op jit(solution)/shard_map/ppermute | solution.py:239
  1615.6 38.3 %grad_w_in.11.dep = f32[640,5120]{1,0:T(8,128)} custom-call(s32[1]{0:T(128)} %bitcast.6.cs, bf16[1280,4096]{1,0:T(8,128)(2,1)} %get-tuple-element.41.ut, bf16[4096,5120]{1,0:T(8,128)(2,1)} %get-tuple-element.42.da_ref, f32[2560,1280]{1,0:T(8,128)} %grad_w_out.11.dep, f32[640,5120]{1,0:T(8,128)} %collective-permute-done.17.refs_0_), custom_call_target="tpu_custom_call" | custom-call | flops 26843545600 | bytes 50000000 | tf_op jit(solution)/shard_map/grad_w_in/pallas_call | solution.py:227
  1653.9 0.0 collective-permute-start.14
  1654.0 0.5 collective-permute-start.15
  1654.5 6.7 dynamic_update_slice.21
  1661.2 6.9 dynamic_update_slice.18
  1668.1 72.9 %grad_x.1 = bf16[4096,1280]{1,0:T(8,128)(2,1)} custom-call(bf16[4096,1280]{1,0:T(8,128)(2,1)} %x_ref.5, bf16[4096,1280]{1,0:T(8,128)(2,1)} %get-tuple-element.35.dy_ref, bf16[4096,5120]{1,0:T(8,128)(2,1)} %get-tuple-element.42.da_ref, bf16[640,5120]{1,0:T(8,128)(2,1)} %bitcast.27, bf16[640,5120]{1,0:T(8,128)(2,1)} %collective-permute-done.10.w1o, ...), custom_call_target="tpu_custom_call" | custom-call | flops 53687091200 | bytes 80000000 | tf_op jit(solution)/shard_map/grad_x/pallas_call | solution.py:176
  1741.0 129.7 %mlp_fwd.5 = bf16[4096,1280]{1,0:T(8,128)(2,1)} custom-call(bf16[4096,1280]{1,0:T(8,128)(2,1)} %mlp_fwd.4.x_ref.dep, bf16[640,5120]{1,0:T(8,128)(2,1)} %all-gather.13.cloned.1.call-done.w1m, bf16[640,5120]{1,0:T(8,128)(2,1)} %collective-permute-done.14.w1o, bf16[2560,1280]{1,0:T(8,128)(2,1)} %all-gather.15.cloned.1.call-done.w2m, ...), custom_call_target="tpu_custom_call" | custom-call | flops 107374182400 | bytes 50000000 | tf_op jit(solution)/shard_map/mlp_fwd/pallas_call | solution.py:84
  1870.8 3.8 bitcast_dynamic-update-slice_fusion.1
  1874.6 3.9 bitcast_dynamic-update-slice_fusion.3
  1878.6 3.8 bitcast_dynamic-update-slice_fusion
  1882.4 3.9 bitcast_dynamic-update-slice_fusion.2
  (35 shorter events, 0.4 us)
Async XLA Ops:
  7.2 74.4 %all-gather.17.cloned.1.call-start = ((), (), s32[]{:S(2)}) async-start(), calls=%async_computation.16 | async-start | bytes 8192000 | tf_op jit(solution)/shard_map/all_gather | solution.py:257
  12.0 138.1 %all-gather.19.cloned.1.call-start = ((), (), s32[]{:S(2)}) async-start(), calls=%async_computation.17 | async-start | bytes 8192000 | tf_op jit(solution)/shard_map/all_gather | solution.py:258
  16.9 202.2 %all-gather.9.cloned.1.call-start = ((), (), s32[]{:S(2)}) async-start(), calls=%async_computation.6 | async-start | bytes 8192000 | tf_op jit(solution)/shard_map/all_gather | solution.py:257
  150.1 137.3 %all-gather.11.cloned.1.call-start = ((), (), s32[]{:S(2)}) async-start(), calls=%async_computation.7 | async-start | bytes 8192000 | tf_op jit(solution)/shard_map/all_gather | solution.py:258
  150.7 285.9 %all-gather.13.cloned.1.call-start = ((), (), s32[]{:S(2)}) async-start(), calls=%async_computation.8 | async-start | bytes 8192000 | tf_op jit(solution)/shard_map/all_gather | solution.py:257
  287.4 149.3 %all-gather.15.cloned.1.call-start = ((), (), s32[]{:S(2)}) async-start(), calls=%async_computation.9 | async-start | bytes 8192000 | tf_op jit(solution)/shard_map/all_gather | solution.py:258
  287.5 10.9 collective-permute-start
  287.5 20.2 %collective-permute-start.1 = (bf16[2560,1280]{1,0:T(8,128)(2,1)}, bf16[2560,1280]{1,0:T(8,128)(2,1)}, u32[]{:S(2)}, u32[]{:S(2)}) collective-permute-start(bf16[2560,1280]{1,0:T(8,128)(2,1)} %bitcast.28), channel_id=1, source_target_pairs={{0,1},{1,0},{2,3},{3,2},{4,5},{5,4},{6,7},{7,6}} | collective-permute-start | bytes 19660808 | tf_op jit(solution)/shard_map/ppermute | solution.py:239
  288.0 1366.4 %reduce-scatter.13.cloned.1.call-start = ((), (), s32[]{:S(2)}) async-start(), calls=%async_computation.13 | async-start | bytes 16384000 | tf_op jit(solution)/shard_map/reduce_scatter | solution.py:282
  288.1 149.1 %collective-permute-start.2 = (bf16[640,5120]{1,0:T(8,128)(2,1)}, bf16[640,5120]{1,0:T(8,128)(2,1)}, u32[]{:S(2)}, u32[]{:S(2)}) collective-permute-start(bf16[640,5120]{1,0:T(8,128)(2,1)} %all-gather.9.cloned.1.call-done.w1m), channel_id=1, source_target_pairs={{0,1},{1,0},{2,3},{3,2},{4,5},{5,4},{6,7},{7,6}} | collective-permute-start | bytes 19660808 | tf_op jit(solution)/shard_map/ppermute | solution.py:239
  288.1 149.0 %collective-permute-start.3 = (bf16[2560,1280]{1,0:T(8,128)(2,1)}, bf16[2560,1280]{1,0:T(8,128)(2,1)}, u32[]{:S(2)}, u32[]{:S(2)}) collective-permute-start(bf16[2560,1280]{1,0:T(8,128)(2,1)} %all-gather.11.cloned.1.call-done.w2m), channel_id=1, source_target_pairs={{0,1},{1,0},{2,3},{3,2},{4,5},{5,4},{6,7},{7,6}} | collective-permute-start | bytes 19660808 | tf_op jit(solution)/shard_map/ppermute | solution.py:239
  436.6 129.9 %collective-permute-start.4 = (bf16[640,5120]{1,0:T(8,128)(2,1)}, bf16[640,5120]{1,0:T(8,128)(2,1)}, u32[]{:S(2)}, u32[]{:S(2)}) collective-permute-start(bf16[640,5120]{1,0:T(8,128)(2,1)} %all-gather.13.cloned.1.call-done.w1m), channel_id=1, source_target_pairs={{0,1},{1,0},{2,3},{3,2},{4,5},{5,4},{6,7},{7,6}} | collective-permute-start | bytes 19660808 | tf_op jit(solution)/shard_map/ppermute | solution.py:239
  436.8 129.8 %collective-permute-start.5 = (bf16[2560,1280]{1,0:T(8,128)(2,1)}, bf16[2560,1280]{1,0:T(8,128)(2,1)}, u32[]{:S(2)}, u32[]{:S(2)}) collective-permute-start(bf16[2560,1280]{1,0:T(8,128)(2,1)} %all-gather.15.cloned.1.call-done.w2m), channel_id=1, source_target_pairs={{0,1},{1,0},{2,3},{3,2},{4,5},{5,4},{6,7},{7,6}} | collective-permute-start | bytes 19660808 | tf_op jit(solution)/shard_map/ppermute | solution.py:239
  820.5 35.4 %collective-permute-start.8 = (f32[2560,1280]{1,0:T(8,128)}, f32[2560,1280]{1,0:T(8,128)}, u32[]{:S(2)}, u32[]{:S(2)}) collective-permute-start(f32[2560,1280]{1,0:T(8,128)} %grad_w_out.6.dep), channel_id=1, source_target_pairs={{0,1},{1,0},{2,3},{3,2},{4,5},{5,4},{6,7},{7,6}} | collective-permute-start | bytes 39321608 | tf_op jit(solution)/shard_map/ppermute | solution.py:239
  892.3 768.9 %reduce-scatter.7.cloned.1.call-start = ((), (), s32[]{:S(2)}) async-start(), calls=%async_computation.10 | async-start | bytes 16384000 | tf_op jit(solution)/shard_map/reduce_scatter | solution.py:284
  892.4 20.3 %collective-permute-start.9 = (f32[640,5120]{1,0:T(8,128)}, f32[640,5120]{1,0:T(8,128)}, u32[]{:S(2)}, u32[]{:S(2)}) collective-permute-start(f32[640,5120]{1,0:T(8,128)} %grad_w_in.6.dep), channel_id=1, source_target_pairs={{0,1},{1,0},{2,3},{3,2},{4,5},{5,4},{6,7},{7,6}} | collective-permute-start | bytes 39321608 | tf_op jit(solution)/shard_map/ppermute | solution.py:239
  892.7 58.3 %collective-permute-start.6 = (bf16[640,5120]{1,0:T(8,128)(2,1)}, bf16[640,5120]{1,0:T(8,128)(2,1)}, u32[]{:S(2)}, u32[]{:S(2)}) collective-permute-start(bf16[640,5120]{1,0:T(8,128)(2,1)} %all-gather.9.cloned.1.call-done.w1m), channel_id=1, source_target_pairs={{0,1},{1,0},{2,3},{3,2},{4,5},{5,4},{6,7},{7,6}} | collective-permute-start | bytes 19660808 | tf_op jit(solution)/shard_map/ppermute | solution.py:239
  892.9 58.2 %collective-permute-start.7 = (bf16[2560,1280]{1,0:T(8,128)(2,1)}, bf16[2560,1280]{1,0:T(8,128)(2,1)}, u32[]{:S(2)}, u32[]{:S(2)}) collective-permute-start(bf16[2560,1280]{1,0:T(8,128)(2,1)} %all-gather.11.cloned.1.call-done.w2m), channel_id=1, source_target_pairs={{0,1},{1,0},{2,3},{3,2},{4,5},{5,4},{6,7},{7,6}} | collective-permute-start | bytes 19660808 | tf_op jit(solution)/shard_map/ppermute | solution.py:239
  951.0 919.8 %reduce-scatter.15.cloned.1.call-start = ((), (), s32[]{:S(2)}) async-start(), calls=%async_computation.14 | async-start | bytes 16384000 | tf_op jit(solution)/shard_map/reduce_scatter | solution.py:282
  1205.6 35.4 %collective-permute-start.12 = (f32[2560,1280]{1,0:T(8,128)}, f32[2560,1280]{1,0:T(8,128)}, u32[]{:S(2)}, u32[]{:S(2)}) collective-permute-start(f32[2560,1280]{1,0:T(8,128)} %grad_w_out.8.dep), channel_id=1, source_target_pairs={{0,1},{1,0},{2,3},{3,2},{4,5},{5,4},{6,7},{7,6}} | collective-permute-start | bytes 39321608 | tf_op jit(solution)/shard_map/ppermute | solution.py:239
  1277.3 597.3 %reduce-scatter.9.cloned.1.call-start = ((), (), s32[]{:S(2)}) async-start(), calls=%async_computation.11 | async-start | bytes 16384000 | tf_op jit(solution)/shard_map/reduce_scatter | solution.py:284
  1277.4 20.3 %collective-permute-start.13 = (f32[640,5120]{1,0:T(8,128)}, f32[640,5120]{1,0:T(8,128)}, u32[]{:S(2)}, u32[]{:S(2)}) collective-permute-start(f32[640,5120]{1,0:T(8,128)} %grad_w_in.8.dep), channel_id=1, source_target_pairs={{0,1},{1,0},{2,3},{3,2},{4,5},{5,4},{6,7},{7,6}} | collective-permute-start | bytes 39321608 | tf_op jit(solution)/shard_map/ppermute | solution.py:239
  1277.7 58.3 %collective-permute-start.10 = (bf16[640,5120]{1,0:T(8,128)(2,1)}, bf16[640,5120]{1,0:T(8,128)(2,1)}, u32[]{:S(2)}, u32[]{:S(2)}) collective-permute-start(bf16[640,5120]{1,0:T(8,128)(2,1)} %bitcast.25), channel_id=1, source_target_pairs={{0,1},{1,0},{2,3},{3,2},{4,5},{5,4},{6,7},{7,6}} | collective-permute-start | bytes 19660808 | tf_op jit(solution)/shard_map/ppermute | solution.py:239
  1277.9 58.1 %collective-permute-start.11 = (bf16[2560,1280]{1,0:T(8,128)(2,1)}, bf16[2560,1280]{1,0:T(8,128)(2,1)}, u32[]{:S(2)}, u32[]{:S(2)}) collective-permute-start(bf16[2560,1280]{1,0:T(8,128)(2,1)} %bitcast.30), channel_id=1, source_target_pairs={{0,1},{1,0},{2,3},{3,2},{4,5},{5,4},{6,7},{7,6}} | collective-permute-start | bytes 19660808 | tf_op jit(solution)/shard_map/ppermute | solution.py:239
  1335.9 542.7 %reduce-scatter.17.cloned.1.call-start = ((), (), s32[]{:S(2)}) async-start(), calls=%async_computation.15 | async-start | bytes 16384000 | tf_op jit(solution)/shard_map/reduce_scatter | solution.py:282
  1523.6 35.4 %collective-permute-start.16 = (f32[2560,1280]{1,0:T(8,128)}, f32[2560,1280]{1,0:T(8,128)}, u32[]{:S(2)}, u32[]{:S(2)}) collective-permute-start(f32[2560,1280]{1,0:T(8,128)} %grad_w_out.10.dep), channel_id=1, source_target_pairs={{0,1},{1,0},{2,3},{3,2},{4,5},{5,4},{6,7},{7,6}} | collective-permute-start | bytes 39321608 | tf_op jit(solution)/shard_map/ppermute | solution.py:239
  1595.2 287.2 %reduce-scatter.11.cloned.1.call-start = ((), (), s32[]{:S(2)}) async-start(), calls=%async_computation.12 | async-start | bytes 16384000 | tf_op jit(solution)/shard_map/reduce_scatter | solution.py:284
  1595.3 20.3 %collective-permute-start.17 = (f32[640,5120]{1,0:T(8,128)}, f32[640,5120]{1,0:T(8,128)}, u32[]{:S(2)}, u32[]{:S(2)}) collective-permute-start(f32[640,5120]{1,0:T(8,128)} %grad_w_in.10.dep), channel_id=1, source_target_pairs={{0,1},{1,0},{2,3},{3,2},{4,5},{5,4},{6,7},{7,6}} | collective-permute-start | bytes 39321608 | tf_op jit(solution)/shard_map/ppermute | solution.py:239
  1653.9 87.1 %collective-permute-start.14 = (bf16[640,5120]{1,0:T(8,128)(2,1)}, bf16[640,5120]{1,0:T(8,128)(2,1)}, u32[]{:S(2)}, u32[]{:S(2)}) collective-permute-start(bf16[640,5120]{1,0:T(8,128)(2,1)} %all-gather.13.cloned.1.call-done.w1m), channel_id=1, source_target_pairs={{0,1},{1,0},{2,3},{3,2},{4,5},{5,4},{6,7},{7,6}} | collective-permute-start | bytes 19660808 | tf_op jit(solution)/shard_map/ppermute | solution.py:239
  1654.0 87.0 %collective-permute-start.15 = (bf16[2560,1280]{1,0:T(8,128)(2,1)}, bf16[2560,1280]{1,0:T(8,128)(2,1)}, u32[]{:S(2)}, u32[]{:S(2)}) collective-permute-start(bf16[2560,1280]{1,0:T(8,128)(2,1)} %all-gather.15.cloned.1.call-done.w2m), channel_id=1, source_target_pairs={{0,1},{1,0},{2,3},{3,2},{4,5},{5,4},{6,7},{7,6}} | collective-permute-start | bytes 19660808 | tf_op jit(solution)/shard_map/ppermute | solution.py:239
Sparse Core Ops, SparseCore 0:
  12.1 69.4 all-gather.16
  83.4 66.6 all-gather.18
  152.4 66.6 all-gather.8
  220.7 66.6 all-gather.10
  289.6 66.6 all-gather.12
  358.5 66.6 all-gather.14
  892.5 119.2 reduce-scatter.12
  1014.9 119.3 reduce-scatter.6
  1277.4 119.3 reduce-scatter.14
  1399.7 119.3 reduce-scatter.8
  1595.3 119.3 reduce-scatter.16
  1717.7 119.2 reduce-scatter.10

commit v2 on v1

--- a/solution.py
+++ b/solution.py
@@ -71,15 +71,21 @@
     x_wide = x_ref[...].astype(jnp.float32)
     u_s[...] = norm_rows(x_wide)[0].astype(jnp.bfloat16)
     acc[...] = x_wide
-    for j in range(F // ch):
-        cols = pl.ds(j * ch, ch)
-        a = jnp.dot(u_s[...], w1v[:, cols], preferred_element_type=jnp.float32).astype(jnp.bfloat16).astype(jnp.float32)
-        s = gelu_fwd(a).astype(jnp.bfloat16)
-        acc[...] += jnp.dot(s, w2v[cols, :], preferred_element_type=jnp.float32)
+
+    def hidden(j):
+        return jnp.dot(u_s[...], w1v[:, pl.ds(j * ch, ch)], preferred_element_type=jnp.float32).astype(jnp.bfloat16)
+
+    n = F // ch
+    held = hidden(0)
+    for j in range(n):
+        ahead = hidden(j + 1) if j + 1 < n else None
+        s = gelu_fwd(held.astype(jnp.float32)).astype(jnp.bfloat16)
+        acc[...] += jnp.dot(s, w2v[pl.ds(j * ch, ch), :], preferred_element_type=jnp.float32)
+        held = ahead
     o_ref[...] = acc[...].astype(jnp.bfloat16)
 
 
-def fwd_call(x, w1m, w1o, w2m, w2o, dep, tm=512, ch=1024):
+def fwd_call(x, w1m, w1o, w2m, w2o, dep, tm=512, ch=1280):
     row = pl.BlockSpec((tm, D), lambda i: (i, 0))
     return pl.pallas_call(
         functools.partial(fwd_kernel, ch), grid=(T // tm,), in_specs=[row] + [ANY] * 5, out_specs=row,
@@ -106,26 +112,37 @@
         ut_ref[...] = u.T
 
     ch = s_ref.shape[1]
-    for k in range(ch // sub):
-        cols = pl.ds(pl.multiple_of(j * ch + k * sub, sub), sub)
-        a = jnp.dot(u_s[...], w1v[:, cols], preferred_element_type=jnp.float32).astype(jnp.bfloat16).astype(jnp.float32)
-        ds = lax.dot_general(dy_ref[...], w2v[cols, :], LAST, preferred_element_type=jnp.float32)
+    n = ch // sub
+    if full:
+        dx_ref, acc = refs[:2]
+
+        @pl.when(j == 0)
+        def _():
+            acc[...] = jnp.zeros_like(acc)
+
+    def cols(k, width):
+        return pl.ds(pl.multiple_of(j * ch + k * sub, sub), width)
+
+    def dots(k):
+        a = jnp.dot(u_s[...], w1v[:, cols(k, sub)], preferred_element_type=jnp.float32).astype(jnp.bfloat16).astype(jnp.float32)
+        return a, lax.dot_general(dy_ref[...], w2v[cols(k, sub), :], LAST, preferred_element_type=jnp.float32)
+
+    def elementwise(k, a, ds):
         s, slope = gelu_both(a)
         s_ref[:, k * sub:(k + 1) * sub] = s.astype(jnp.bfloat16)
         da_ref[:, k * sub:(k + 1) * sub] = (slope * ds).astype(jnp.bfloat16)
+
+    def add_du(k, width):
+        acc[...] += lax.dot_general(da_ref[:, k * sub:k * sub + width], w1v[:, cols(k, width)], LAST, preferred_element_type=jnp.float32)
+
+    held = dots(0)
+    for k in range(1, n + 1):
+        ahead = dots(k) if k < n else None
+        elementwise(k - 1, *held)
+        held = ahead
     if not full:
         return
-    dx_ref, acc = refs[:2]
-    cols = pl.ds(pl.multiple_of(j * ch, ch), ch)
-    du = lax.dot_general(da_ref[...], w1v[:, cols], LAST, preferred_element_type=jnp.float32)
-
-    @pl.when(j == 0)
-    def _():
-        acc[...] = du
-
-    @pl.when(j > 0)
-    def _():
-        acc[...] += du
+    add_du(0, ch)
 
     @pl.when(j == pl.num_programs(1) - 1)
     def _():
@@ -259,11 +276,12 @@
             return g1, g2
 
         kept = [gather(0, ())]
+        first = swap(kept[0][0])
         xs = [x_rows]
         for l in range(LAYERS - 1):
-            kept.append(gather(l + 1, kept[-1]))
+            kept.append(gather(l + 1, kept[-1] + ((first,) if l == 0 else ())))
             w1, w2 = kept[l]
-            w1o, w2o = swap(w1), swap(w2)
+            w1o, w2o = swap(w1) if l else first, swap(w2)
             xs.append(fwd_call(xs[-1], w1, w1o, w2, w2o, x_rows))
         grad = grad_rows
         tok = xs[-1]

time: 1900 us -> 1880 us (0.989)
  transfers between devices with their start and end apart: 30 -> 30, of which waited for: 9 -> 8; matrix products, arithmetic and copies ran while one was open for 2% -> 2% of each run, Pallas kernels for 63% -> 63%
where the time goes in v2:
time: 1880 us; the launch traced here: 1870 us
  Pallas kernels  1480 us (79%)
  waiting for transfers between devices  340 us (18%)
  local copies, waits for them, and re-layouts  38.8 us (2%)
    pallas_call x3, Pallas kernels, bwd_call(): pl.pallas_call(functools.partial(bwd_kernel, sub, full), grid=(T // tm, F...  586 us
    pallas_call x3, Pallas kernels, fwd_call(): pl.pallas_call(functools.partial(fwd_kernel, ch), grid=(T // tm,), in_spe...  381 us
    pallas_call x6, Pallas kernels, win_call(): pl.pallas_call(win_kernel, grid_spec=spec, out_shape=jax.ShapeDtypeStruct...  221 us
    pallas_call x6, Pallas kernels, wout_call(): pl.pallas_call(wout_kernel, grid_spec=spec, out_shape=jax.ShapeDtypeStruc...  216 us
    all_gather x3, waiting for transfers between devices, gather(): g2 = lax.all_gather(p2, CHIPS, axis=0, tiled=True)  137 us
    all_gather x3, waiting for transfers between devices, gather(): g1 = lax.all_gather(p1, CHIPS, axis=0, tiled=True)  133 us
    pallas_call x1, Pallas kernels, du_call(): pl.pallas_call(du_kernel, grid=(T // tm,), in_specs=[row, row, pl.BlockSp...  72.9 us
    ppermute x18, waiting for transfers between devices, swap(): return lax.ppermute(v, 'c', SWAP)  68.6 us
  transfers between devices with their start and end apart: 30, of which 8 were waited for; matrix products, arithmetic and copies ran while one was open for 2% of the time, Pallas kernels for 63%

profile of v2, /device:TPU:0, one launch (start us, length us, event | category | flops | bytes accessed | tf_op | source)
XLA Modules:
  0.0 1874.2 jit_solution(13258309240775740820)
XLA Ops:
  7.2 0.0 all-gather.17.cloned.1.call-start
  7.2 4.8 slice_bitcast_fusion.1
  12.0 0.0 all-gather.19.cloned.1.call-start
  12.1 4.8 slice_bitcast_fusion
  16.9 0.0 all-gather.9.cloned.1.call-start
  16.9 64.7 %all-gather.17.cloned.1.call-done = bf16[1,640,5120]{2,1,0:T(8,128)(2,1)} async-done(((bf16[1,160,5120]{2,1,0:T(8,128)(2,1)}), bf16[1,640,5120]{2,1,0:T(8,128)(2,1)}) %all-gather.17.cloned.1.call-update) | async-done | bytes 6553616 | tf_op jit(solution)/shard_map/all_gather | solution.py:274
  81.6 68.5 %all-gather.19.cloned.1.call-done = bf16[1,2560,1280]{2,1,0:T(8,128)(2,1)} async-done(((bf16[1,640,1280]{2,1,0:T(8,128)(2,1)}), bf16[1,2560,1280]{2,1,0:T(8,128)(2,1)}) %all-gather.19.cloned.1.call-update) | async-done | bytes 6553616 | tf_op jit(solution)/shard_map/all_gather | solution.py:275
  150.1 0.0 all-gather.11.cloned.1.call-start
  150.1 0.5 all-gather.11.cloned.1.call-update
  150.7 0.0 all-gather.13.cloned.1.call-start
  150.7 68.4 %all-gather.9.cloned.1.call-done.w1m = bf16[640,5120]{1,0:T(8,128)(2,1)} async-done(((bf16[160,5120]{1,0:T(8,128)(2,1)}), bf16[640,5120]{1,0:T(8,128)(2,1)}) %all-gather.9.cloned.1.call-update) | async-done | bytes 6553616 | tf_op jit(solution)/shard_map/all_gather | solution.py:274
  219.1 68.3 %all-gather.11.cloned.1.call-done.w2m = bf16[2560,1280]{1,0:T(8,128)(2,1)} async-done(((bf16[640,1280]{1,0:T(8,128)(2,1)}), bf16[2560,1280]{1,0:T(8,128)(2,1)}) %all-gather.11.cloned.1.call-update) | async-done | bytes 6553616 | tf_op jit(solution)/shard_map/all_gather | solution.py:275
  287.4 0.0 all-gather.15.cloned.1.call-start
  287.5 0.5 all-gather.15.cloned.1.call-update
  288.0 0.0 reduce-scatter.13.cloned.1.call-start
  288.1 0.0 collective-permute-start.2
  288.1 0.5 collective-permute-start.3
  288.6 9.8 collective-permute-done.1.w2o
  298.4 126.9 %mlp_fwd.3.x_ref = bf16[4096,1280]{1,0:T(8,128)(2,1)} custom-call(bf16[4096,1280]{1,0:T(8,128)(2,1)} %x_ref.5, bf16[640,5120]{1,0:T(8,128)(2,1)} %bitcast.24, bf16[640,5120]{1,0:T(8,128)(2,1)} %collective-permute-done.w1o, bf16[2560,1280]{1,0:T(8,128)(2,1)} %bitcast.29, bf16[2560,1280]{1,0:T(8,128)(2,1)} %collective-permute-done.1.w2o, bf16[4096,1280]{1,0:T(8,128)(2,1)} %x_ref.5), custom_call_target="tpu_custom_call" | custom-call | flops 107374182400 | bytes 50000000 | tf_op jit(solution)/shard_map/mlp_fwd/pallas_call | solution.py:90
  425.3 0.2 collective-permute-start.4
  425.5 0.4 collective-permute-start.5
  425.9 126.7 %mlp_fwd.4.x_ref.dep = bf16[4096,1280]{1,0:T(8,128)(2,1)} custom-call(bf16[4096,1280]{1,0:T(8,128)(2,1)} %mlp_fwd.3.x_ref, bf16[640,5120]{1,0:T(8,128)(2,1)} %all-gather.9.cloned.1.call-done.w1m, bf16[640,5120]{1,0:T(8,128)(2,1)} %collective-permute-done.2.w1o, bf16[2560,1280]{1,0:T(8,128)(2,1)} %all-gather.11.cloned.1.call-done.w2m, ...), custom_call_target="tpu_custom_call" | custom-call | flops 107374182400 | bytes 50000000 | tf_op jit(solution)/shard_map/mlp_fwd/pallas_call | solution.py:90
  552.6 216.9 %mlp_bwd.3 = (bf16[4096,5120]{1,0:T(8,128)(2,1)}, bf16[4096,5120]{1,0:T(8,128)(2,1)}, bf16[1280,4096]{1,0:T(8,128)(2,1)}, bf16[4096,1280]{1,0:T(8,128)(2,1)}) custom-call(bf16[4096,1280]{1,0:T(8,128)(2,1)} %mlp_fwd.4.x_ref.dep, bf16[4096,1280]{1,0:T(8,128)(2,1)} %dy_ref.5, bf16[640,5120]{1,0:T(8,128)(2,1)} %all-gather.13.cloned.1.call-done.w1m, ...), custom_call_target="tpu_custom_call" | custom-call | flops 161061273600 | bytes 150000000 | tf_op jit(solution)/shard_map/mlp_bwd/pallas_call | solution.py:162
  769.5 35.6 %grad_w_out.6.dep = f32[2560,1280]{1,0:T(8,128)} custom-call(s32[1]{0:T(128)S(6)} %sub.3.cs, bf16[4096,5120]{1,0:T(8,128)(2,1)} %get-tuple-element.34.s_ref, bf16[4096,1280]{1,0:T(8,128)(2,1)} %dy_ref.5, bf16[4096,1280]{1,0:T(8,128)(2,1)} %mlp_fwd.4.x_ref.dep), custom_call_target="tpu_custom_call" | custom-call | flops 26843545600 | bytes 50000000 | tf_op jit(solution)/shard_map/grad_w_out/pallas_call | solution.py:215
  805.1 0.2 collective-permute-start.8
  805.3 35.2 %grad_w_in.6.dep = f32[640,5120]{1,0:T(8,128)} custom-call(s32[1]{0:T(128)S(6)} %sub.3.cs, bf16[1280,4096]{1,0:T(8,128)(2,1)} %get-tuple-element.32.ut, bf16[4096,5120]{1,0:T(8,128)(2,1)} %get-tuple-element.33.da_ref, f32[2560,1280]{1,0:T(8,128)} %grad_w_out.6.dep), custom_call_target="tpu_custom_call" | custom-call | flops 26843545600 | bytes 50000000 | tf_op jit(solution)/shard_map/grad_w_in/pallas_call | solution.py:244
  840.5 36.4 %grad_w_out.7.dep = f32[2560,1280]{1,0:T(8,128)} custom-call(s32[1]{0:T(128)} %bitcast.6.cs, bf16[4096,5120]{1,0:T(8,128)(2,1)} %get-tuple-element.34.s_ref, bf16[4096,1280]{1,0:T(8,128)(2,1)} %dy_ref.5, f32[640,5120]{1,0:T(8,128)} %grad_w_in.6.dep, f32[2560,1280]{1,0:T(8,128)} %collective-permute-done.8.refs_0_), custom_call_target="tpu_custom_call" | custom-call | flops 26843545600 | bytes 50000000 | tf_op jit(solution)/shard_map/grad_w_out/pallas_call | solution.py:215
  876.9 0.0 reduce-scatter.7.cloned.1.call-start
  876.9 0.3 collective-permute-start.9
  877.2 0.2 collective-permute-start.6
  877.5 0.3 collective-permute-start.7
  877.8 19.5 %collective-permute-done.9.refs_0_ = f32[640,5120]{1,0:T(8,128)} collective-permute-done((f32[640,5120]{1,0:T(8,128)}, f32[640,5120]{1,0:T(8,128)}, u32[]{:S(2)}, u32[]{:S(2)}) %collective-permute-start.9) | collective-permute-done | bytes 13107232 | tf_op jit(solution)/shard_map/ppermute | solution.py:256
  897.2 38.4 %grad_w_in.7.dep = f32[640,5120]{1,0:T(8,128)} custom-call(s32[1]{0:T(128)} %bitcast.6.cs, bf16[1280,4096]{1,0:T(8,128)(2,1)} %get-tuple-element.32.ut, bf16[4096,5120]{1,0:T(8,128)(2,1)} %get-tuple-element.33.da_ref, f32[2560,1280]{1,0:T(8,128)} %grad_w_out.7.dep, f32[640,5120]{1,0:T(8,128)} %collective-permute-done.9.refs_0_), custom_call_target="tpu_custom_call" | custom-call | flops 26843545600 | bytes 50000000 | tf_op jit(solution)/shard_map/grad_w_in/pallas_call | solution.py:244
  935.6 0.0 reduce-scatter.15.cloned.1.call-start
  935.7 217.4 %mlp_bwd.4 = (bf16[4096,5120]{1,0:T(8,128)(2,1)}, bf16[4096,5120]{1,0:T(8,128)(2,1)}, bf16[1280,4096]{1,0:T(8,128)(2,1)}, bf16[4096,1280]{1,0:T(8,128)(2,1)}) custom-call(bf16[4096,1280]{1,0:T(8,128)(2,1)} %mlp_fwd.3.x_ref, bf16[4096,1280]{1,0:T(8,128)(2,1)} %get-tuple-element.29.dy_ref, bf16[640,5120]{1,0:T(8,128)(2,1)} %all-gather.9.cloned.1.call-done.w1m, ...), custom_call_target="tpu_custom_call" | custom-call | flops 161061273600 | bytes 150000000 | tf_op jit(solution)/shard_map/mlp_bwd/pallas_call | solution.py:162
  1153.1 35.4 %grad_w_out.8.dep = f32[2560,1280]{1,0:T(8,128)} custom-call(s32[1]{0:T(128)S(6)} %sub.3.cs, bf16[4096,5120]{1,0:T(8,128)(2,1)} %get-tuple-element.40.s_ref, bf16[4096,1280]{1,0:T(8,128)(2,1)} %get-tuple-element.29.dy_ref, f32[640,5120]{1,0:T(8,128)} %grad_w_in.7.dep), custom_call_target="tpu_custom_call" | custom-call | flops 26843545600 | bytes 50000000 | tf_op jit(solution)/shard_map/grad_w_out/pallas_call | solution.py:215
  1188.5 0.2 collective-permute-start.12
  1188.7 35.2 %grad_w_in.8.dep = f32[640,5120]{1,0:T(8,128)} custom-call(s32[1]{0:T(128)S(6)} %sub.3.cs, bf16[1280,4096]{1,0:T(8,128)(2,1)} %get-tuple-element.38.ut, bf16[4096,5120]{1,0:T(8,128)(2,1)} %get-tuple-element.39.da_ref, f32[2560,1280]{1,0:T(8,128)} %grad_w_out.8.dep), custom_call_target="tpu_custom_call" | custom-call | flops 26843545600 | bytes 50000000 | tf_op jit(solution)/shard_map/grad_w_in/pallas_call | solution.py:244
  1223.9 36.3 %grad_w_out.9.dep = f32[2560,1280]{1,0:T(8,128)} custom-call(s32[1]{0:T(128)} %bitcast.6.cs, bf16[4096,5120]{1,0:T(8,128)(2,1)} %get-tuple-element.40.s_ref, bf16[4096,1280]{1,0:T(8,128)(2,1)} %get-tuple-element.29.dy_ref, f32[640,5120]{1,0:T(8,128)} %grad_w_in.8.dep, f32[2560,1280]{1,0:T(8,128)} %collective-permute-done.12.refs_0_), custom_call_target="tpu_custom_call" | custom-call | flops 26843545600 | bytes 50000000 | tf_op jit(solution)/shard_map/grad_w_out/pallas_call | solution.py:215
  1260.2 0.0 reduce-scatter.9.cloned.1.call-start
  1260.3 0.3 collective-permute-start.13
  1260.6 0.2 collective-permute-start.10
  1260.8 0.3 collective-permute-start.11
  1261.1 19.5 %collective-permute-done.13.refs_0_ = f32[640,5120]{1,0:T(8,128)} collective-permute-done((f32[640,5120]{1,0:T(8,128)}, f32[640,5120]{1,0:T(8,128)}, u32[]{:S(2)}, u32[]{:S(2)}) %collective-permute-start.13) | collective-permute-done | bytes 13107232 | tf_op jit(solution)/shard_map/ppermute | solution.py:256
  1280.5 38.3 %grad_w_in.9.dep = f32[640,5120]{1,0:T(8,128)} custom-call(s32[1]{0:T(128)} %bitcast.6.cs, bf16[1280,4096]{1,0:T(8,128)(2,1)} %get-tuple-element.38.ut, bf16[4096,5120]{1,0:T(8,128)(2,1)} %get-tuple-element.39.da_ref, f32[2560,1280]{1,0:T(8,128)} %grad_w_out.9.dep, f32[640,5120]{1,0:T(8,128)} %collective-permute-done.13.refs_0_), custom_call_target="tpu_custom_call" | custom-call | flops 26843545600 | bytes 50000000 | tf_op jit(solution)/shard_map/grad_w_in/pallas_call | solution.py:244
  1318.9 0.0 reduce-scatter.17.cloned.1.call-start
  1318.9 151.5 %mlp_bwd.5 = (bf16[4096,5120]{1,0:T(8,128)(2,1)}, bf16[4096,5120]{1,0:T(8,128)(2,1)}, bf16[1280,4096]{1,0:T(8,128)(2,1)}) custom-call(bf16[4096,1280]{1,0:T(8,128)(2,1)} %x_ref.5, bf16[4096,1280]{1,0:T(8,128)(2,1)} %get-tuple-element.35.dy_ref, bf16[640,5120]{1,0:T(8,128)(2,1)} %bitcast.26, bf16[640,5120]{1,0:T(8,128)(2,1)} %collective-permute-done.10.w1o, ...), custom_call_target="tpu_custom_call" | custom-call | flops 107374182400 | bytes 150000000 | tf_op jit(solution)/shard_map/mlp_bwd/pallas_call | solution.py:162
  1470.5 35.9 %grad_w_out.10.dep = f32[2560,1280]{1,0:T(8,128)} custom-call(s32[1]{0:T(128)S(6)} %sub.3.cs, bf16[4096,5120]{1,0:T(8,128)(2,1)} %get-tuple-element.43.s_ref, bf16[4096,1280]{1,0:T(8,128)(2,1)} %get-tuple-element.35.dy_ref, f32[640,5120]{1,0:T(8,128)} %grad_w_in.9.dep), custom_call_target="tpu_custom_call" | custom-call | flops 26843545600 | bytes 50000000 | tf_op jit(solution)/shard_map/grad_w_out/pallas_call | solution.py:215
  1506.4 0.1 collective-permute-start.16
  1506.5 35.3 %grad_w_in.10.dep = f32[640,5120]{1,0:T(8,128)} custom-call(s32[1]{0:T(128)S(6)} %sub.3.cs, bf16[1280,4096]{1,0:T(8,128)(2,1)} %get-tuple-element.41.ut, bf16[4096,5120]{1,0:T(8,128)(2,1)} %get-tuple-element.42.da_ref, f32[2560,1280]{1,0:T(8,128)} %grad_w_out.10.dep), custom_call_target="tpu_custom_call" | custom-call | flops 26843545600 | bytes 50000000 | tf_op jit(solution)/shard_map/grad_w_in/pallas_call | solution.py:244
  1541.8 36.2 %grad_w_out.11.dep = f32[2560,1280]{1,0:T(8,128)} custom-call(s32[1]{0:T(128)} %bitcast.6.cs, bf16[4096,5120]{1,0:T(8,128)(2,1)} %get-tuple-element.43.s_ref, bf16[4096,1280]{1,0:T(8,128)(2,1)} %get-tuple-element.35.dy_ref, f32[640,5120]{1,0:T(8,128)} %grad_w_in.10.dep, f32[2560,1280]{1,0:T(8,128)} %collective-permute-done.16.refs_0_), custom_call_target="tpu_custom_call" | custom-call | flops 26843545600 | bytes 50000000 | tf_op jit(solution)/shard_map/grad_w_out/pallas_call | solution.py:215
  1578.0 0.0 reduce-scatter.11.cloned.1.call-start
  1578.1 0.4 collective-permute-start.17
  1578.5 19.9 %collective-permute-done.17.refs_0_ = f32[640,5120]{1,0:T(8,128)} collective-permute-done((f32[640,5120]{1,0:T(8,128)}, f32[640,5120]{1,0:T(8,128)}, u32[]{:S(2)}, u32[]{:S(2)}) %collective-permute-start.17) | collective-permute-done | bytes 13107232 | tf_op jit(solution)/shard_map/ppermute | solution.py:256
  1598.4 38.3 %grad_w_in.11.dep = f32[640,5120]{1,0:T(8,128)} custom-call(s32[1]{0:T(128)} %bitcast.6.cs, bf16[1280,4096]{1,0:T(8,128)(2,1)} %get-tuple-element.41.ut, bf16[4096,5120]{1,0:T(8,128)(2,1)} %get-tuple-element.42.da_ref, f32[2560,1280]{1,0:T(8,128)} %grad_w_out.11.dep, f32[640,5120]{1,0:T(8,128)} %collective-permute-done.17.refs_0_), custom_call_target="tpu_custom_call" | custom-call | flops 26843545600 | bytes 50000000 | tf_op jit(solution)/shard_map/grad_w_in/pallas_call | solution.py:244
  1636.8 0.5 collective-permute-start.15
  1637.3 6.7 dynamic_update_slice.21
  1644.0 6.9 dynamic_update_slice.18
  1651.0 72.9 %grad_x.1 = bf16[4096,1280]{1,0:T(8,128)(2,1)} custom-call(bf16[4096,1280]{1,0:T(8,128)(2,1)} %x_ref.5, bf16[4096,1280]{1,0:T(8,128)(2,1)} %get-tuple-element.35.dy_ref, bf16[4096,5120]{1,0:T(8,128)(2,1)} %get-tuple-element.42.da_ref, bf16[640,5120]{1,0:T(8,128)(2,1)} %bitcast.27, bf16[640,5120]{1,0:T(8,128)(2,1)} %collective-permute-done.10.w1o, ...), custom_call_target="tpu_custom_call" | custom-call | flops 53687091200 | bytes 80000000 | tf_op jit(solution)/shard_map/grad_x/pallas_call | solution.py:193
  1723.8 127.5 %mlp_fwd.5 = bf16[4096,1280]{1,0:T(8,128)(2,1)} custom-call(bf16[4096,1280]{1,0:T(8,128)(2,1)} %mlp_fwd.4.x_ref.dep, bf16[640,5120]{1,0:T(8,128)(2,1)} %all-gather.13.cloned.1.call-done.w1m, bf16[640,5120]{1,0:T(8,128)(2,1)} %collective-permute-done.14.w1o, bf16[2560,1280]{1,0:T(8,128)(2,1)} %all-gather.15.cloned.1.call-done.w2m, ...), custom_call_target="tpu_custom_call" | custom-call | flops 107374182400 | bytes 50000000 | tf_op jit(solution)/shard_map/mlp_fwd/pallas_call | solution.py:90
  1851.4 3.8 bitcast_dynamic-update-slice_fusion.1
  1855.3 3.9 bitcast_dynamic-update-slice_fusion.3
  1859.2 3.8 bitcast_dynamic-update-slice_fusion
  1863.1 3.9 bitcast_dynamic-update-slice_fusion.2
  (35 shorter events, 0.3 us)
Async XLA Ops:
  7.2 74.4 %all-gather.17.cloned.1.call-start = ((), (), s32[]{:S(2)}) async-start(), calls=%async_computation.16 | async-start | bytes 8192000 | tf_op jit(solution)/shard_map/all_gather | solution.py:274
  12.0 138.1 %all-gather.19.cloned.1.call-start = ((), (), s32[]{:S(2)}) async-start(), calls=%async_computation.17 | async-start | bytes 8192000 | tf_op jit(solution)/shard_map/all_gather | solution.py:275
  16.9 202.2 %all-gather.9.cloned.1.call-start = ((), (), s32[]{:S(2)}) async-start(), calls=%async_computation.6 | async-start | bytes 8192000 | tf_op jit(solution)/shard_map/all_gather | solution.py:274
  81.6 68.5 %collective-permute-start = (bf16[640,5120]{1,0:T(8,128)(2,1)}, bf16[640,5120]{1,0:T(8,128)(2,1)}, u32[]{:S(2)}, u32[]{:S(2)}) collective-permute-start(bf16[640,5120]{1,0:T(8,128)(2,1)} %bitcast.23), channel_id=1, source_target_pairs={{0,1},{1,0},{2,3},{3,2},{4,5},{5,4},{6,7},{7,6}} | collective-permute-start | bytes 19660808 | tf_op jit(solution)/shard_map/ppermute | solution.py:256
  150.1 137.3 %all-gather.11.cloned.1.call-start = ((), (), s32[]{:S(2)}) async-start(), calls=%async_computation.7 | async-start | bytes 8192000 | tf_op jit(solution)/shard_map/all_gather | solution.py:275
  150.7 274.7 %all-gather.13.cloned.1.call-start = ((), (), s32[]{:S(2)}) async-start(), calls=%async_computation.8 | async-start | bytes 8192000 | tf_op jit(solution)/shard_map/all_gather | solution.py:274
  287.4 138.1 %all-gather.15.cloned.1.call-start = ((), (), s32[]{:S(2)}) async-start(), calls=%async_computation.9 | async-start | bytes 8192000 | tf_op jit(solution)/shard_map/all_gather | solution.py:275
  287.5 10.9 collective-permute-start.1
  288.0 1349.3 %reduce-scatter.13.cloned.1.call-start = ((), (), s32[]{:S(2)}) async-start(), calls=%async_computation.13 | async-start | bytes 16384000 | tf_op jit(solution)/shard_map/reduce_scatter | solution.py:300
  288.1 137.8 %collective-permute-start.2 = (bf16[640,5120]{1,0:T(8,128)(2,1)}, bf16[640,5120]{1,0:T(8,128)(2,1)}, u32[]{:S(2)}, u32[]{:S(2)}) collective-permute-start(bf16[640,5120]{1,0:T(8,128)(2,1)} %all-gather.9.cloned.1.call-done.w1m), channel_id=1, source_target_pairs={{0,1},{1,0},{2,3},{3,2},{4,5},{5,4},{6,7},{7,6}} | collective-permute-start | bytes 19660808 | tf_op jit(solution)/shard_map/ppermute | solution.py:256
  288.1 137.8 %collective-permute-start.3 = (bf16[2560,1280]{1,0:T(8,128)(2,1)}, bf16[2560,1280]{1,0:T(8,128)(2,1)}, u32[]{:S(2)}, u32[]{:S(2)}) collective-permute-start(bf16[2560,1280]{1,0:T(8,128)(2,1)} %all-gather.11.cloned.1.call-done.w2m), channel_id=1, source_target_pairs={{0,1},{1,0},{2,3},{3,2},{4,5},{5,4},{6,7},{7,6}} | collective-permute-start | bytes 19660808 | tf_op jit(solution)/shard_map/ppermute | solution.py:256
  425.3 127.2 %collective-permute-start.4 = (bf16[640,5120]{1,0:T(8,128)(2,1)}, bf16[640,5120]{1,0:T(8,128)(2,1)}, u32[]{:S(2)}, u32[]{:S(2)}) collective-permute-start(bf16[640,5120]{1,0:T(8,128)(2,1)} %all-gather.13.cloned.1.call-done.w1m), channel_id=1, source_target_pairs={{0,1},{1,0},{2,3},{3,2},{4,5},{5,4},{6,7},{7,6}} | collective-permute-start | bytes 19660808 | tf_op jit(solution)/shard_map/ppermute | solution.py:256
  425.5 127.1 %collective-permute-start.5 = (bf16[2560,1280]{1,0:T(8,128)(2,1)}, bf16[2560,1280]{1,0:T(8,128)(2,1)}, u32[]{:S(2)}, u32[]{:S(2)}) collective-permute-start(bf16[2560,1280]{1,0:T(8,128)(2,1)} %all-gather.15.cloned.1.call-done.w2m), channel_id=1, source_target_pairs={{0,1},{1,0},{2,3},{3,2},{4,5},{5,4},{6,7},{7,6}} | collective-permute-start | bytes 19660808 | tf_op jit(solution)/shard_map/ppermute | solution.py:256
  805.1 35.4 %collective-permute-start.8 = (f32[2560,1280]{1,0:T(8,128)}, f32[2560,1280]{1,0:T(8,128)}, u32[]{:S(2)}, u32[]{:S(2)}) collective-permute-start(f32[2560,1280]{1,0:T(8,128)} %grad_w_out.6.dep), channel_id=1, source_target_pairs={{0,1},{1,0},{2,3},{3,2},{4,5},{5,4},{6,7},{7,6}} | collective-permute-start | bytes 39321608 | tf_op jit(solution)/shard_map/ppermute | solution.py:256
  876.9 767.1 %reduce-scatter.7.cloned.1.call-start = ((), (), s32[]{:S(2)}) async-start(), calls=%async_computation.10 | async-start | bytes 16384000 | tf_op jit(solution)/shard_map/reduce_scatter | solution.py:302
  876.9 20.3 %collective-permute-start.9 = (f32[640,5120]{1,0:T(8,128)}, f32[640,5120]{1,0:T(8,128)}, u32[]{:S(2)}, u32[]{:S(2)}) collective-permute-start(f32[640,5120]{1,0:T(8,128)} %grad_w_in.6.dep), channel_id=1, source_target_pairs={{0,1},{1,0},{2,3},{3,2},{4,5},{5,4},{6,7},{7,6}} | collective-permute-start | bytes 39321608 | tf_op jit(solution)/shard_map/ppermute | solution.py:256
  877.2 58.4 %collective-permute-start.6 = (bf16[640,5120]{1,0:T(8,128)(2,1)}, bf16[640,5120]{1,0:T(8,128)(2,1)}, u32[]{:S(2)}, u32[]{:S(2)}) collective-permute-start(bf16[640,5120]{1,0:T(8,128)(2,1)} %all-gather.9.cloned.1.call-done.w1m), channel_id=1, source_target_pairs={{0,1},{1,0},{2,3},{3,2},{4,5},{5,4},{6,7},{7,6}} | collective-permute-start | bytes 19660808 | tf_op jit(solution)/shard_map/ppermute | solution.py:256
  877.5 58.2 %collective-permute-start.7 = (bf16[2560,1280]{1,0:T(8,128)(2,1)}, bf16[2560,1280]{1,0:T(8,128)(2,1)}, u32[]{:S(2)}, u32[]{:S(2)}) collective-permute-start(bf16[2560,1280]{1,0:T(8,128)(2,1)} %all-gather.11.cloned.1.call-done.w2m), channel_id=1, source_target_pairs={{0,1},{1,0},{2,3},{3,2},{4,5},{5,4},{6,7},{7,6}} | collective-permute-start | bytes 19660808 | tf_op jit(solution)/shard_map/ppermute | solution.py:256
  935.6 915.8 %reduce-scatter.15.cloned.1.call-start = ((), (), s32[]{:S(2)}) async-start(), calls=%async_computation.14 | async-start | bytes 16384000 | tf_op jit(solution)/shard_map/reduce_scatter | solution.py:300
  1188.5 35.4 %collective-permute-start.12 = (f32[2560,1280]{1,0:T(8,128)}, f32[2560,1280]{1,0:T(8,128)}, u32[]{:S(2)}, u32[]{:S(2)}) collective-permute-start(f32[2560,1280]{1,0:T(8,128)} %grad_w_out.8.dep), channel_id=1, source_target_pairs={{0,1},{1,0},{2,3},{3,2},{4,5},{5,4},{6,7},{7,6}} | collective-permute-start | bytes 39321608 | tf_op jit(solution)/shard_map/ppermute | solution.py:256
  1260.2 595.0 %reduce-scatter.9.cloned.1.call-start = ((), (), s32[]{:S(2)}) async-start(), calls=%async_computation.11 | async-start | bytes 16384000 | tf_op jit(solution)/shard_map/reduce_scatter | solution.py:302
  1260.3 20.3 %collective-permute-start.13 = (f32[640,5120]{1,0:T(8,128)}, f32[640,5120]{1,0:T(8,128)}, u32[]{:S(2)}, u32[]{:S(2)}) collective-permute-start(f32[640,5120]{1,0:T(8,128)} %grad_w_in.8.dep), channel_id=1, source_target_pairs={{0,1},{1,0},{2,3},{3,2},{4,5},{5,4},{6,7},{7,6}} | collective-permute-start | bytes 39321608 | tf_op jit(solution)/shard_map/ppermute | solution.py:256
  1260.6 58.4 %collective-permute-start.10 = (bf16[640,5120]{1,0:T(8,128)(2,1)}, bf16[640,5120]{1,0:T(8,128)(2,1)}, u32[]{:S(2)}, u32[]{:S(2)}) collective-permute-start(bf16[640,5120]{1,0:T(8,128)(2,1)} %bitcast.25), channel_id=1, source_target_pairs={{0,1},{1,0},{2,3},{3,2},{4,5},{5,4},{6,7},{7,6}} | collective-permute-start | bytes 19660808 | tf_op jit(solution)/shard_map/ppermute | solution.py:256
  1260.8 58.1 %collective-permute-start.11 = (bf16[2560,1280]{1,0:T(8,128)(2,1)}, bf16[2560,1280]{1,0:T(8,128)(2,1)}, u32[]{:S(2)}, u32[]{:S(2)}) collective-permute-start(bf16[2560,1280]{1,0:T(8,128)(2,1)} %bitcast.30), channel_id=1, source_target_pairs={{0,1},{1,0},{2,3},{3,2},{4,5},{5,4},{6,7},{7,6}} | collective-permute-start | bytes 19660808 | tf_op jit(solution)/shard_map/ppermute | solution.py:256
  1318.9 540.4 %reduce-scatter.17.cloned.1.call-start = ((), (), s32[]{:S(2)}) async-start(), calls=%async_computation.15 | async-start | bytes 16384000 | tf_op jit(solution)/shard_map/reduce_scatter | solution.py:300
  1506.4 35.4 %collective-permute-start.16 = (f32[2560,1280]{1,0:T(8,128)}, f32[2560,1280]{1,0:T(8,128)}, u32[]{:S(2)}, u32[]{:S(2)}) collective-permute-start(f32[2560,1280]{1,0:T(8,128)} %grad_w_out.10.dep), channel_id=1, source_target_pairs={{0,1},{1,0},{2,3},{3,2},{4,5},{5,4},{6,7},{7,6}} | collective-permute-start | bytes 39321608 | tf_op jit(solution)/shard_map/ppermute | solution.py:256
  1578.0 285.0 %reduce-scatter.11.cloned.1.call-start = ((), (), s32[]{:S(2)}) async-start(), calls=%async_computation.12 | async-start | bytes 16384000 | tf_op jit(solution)/shard_map/reduce_scatter | solution.py:302
  1578.1 20.3 %collective-permute-start.17 = (f32[640,5120]{1,0:T(8,128)}, f32[640,5120]{1,0:T(8,128)}, u32[]{:S(2)}, u32[]{:S(2)}) collective-permute-start(f32[640,5120]{1,0:T(8,128)} %grad_w_in.10.dep), channel_id=1, source_target_pairs={{0,1},{1,0},{2,3},{3,2},{4,5},{5,4},{6,7},{7,6}} | collective-permute-start | bytes 39321608 | tf_op jit(solution)/shard_map/ppermute | solution.py:256
  1636.8 87.1 %collective-permute-start.14 = (bf16[640,5120]{1,0:T(8,128)(2,1)}, bf16[640,5120]{1,0:T(8,128)(2,1)}, u32[]{:S(2)}, u32[]{:S(2)}) collective-permute-start(bf16[640,5120]{1,0:T(8,128)(2,1)} %all-gather.13.cloned.1.call-done.w1m), channel_id=1, source_target_pairs={{0,1},{1,0},{2,3},{3,2},{4,5},{5,4},{6,7},{7,6}} | collective-permute-start | bytes 19660808 | tf_op jit(solution)/shard_map/ppermute | solution.py:256
  1636.8 87.0 %collective-permute-start.15 = (bf16[2560,1280]{1,0:T(8,128)(2,1)}, bf16[2560,1280]{1,0:T(8,128)(2,1)}, u32[]{:S(2)}, u32[]{:S(2)}) collective-permute-start(bf16[2560,1280]{1,0:T(8,128)(2,1)} %all-gather.15.cloned.1.call-done.w2m), channel_id=1, source_target_pairs={{0,1},{1,0},{2,3},{3,2},{4,5},{5,4},{6,7},{7,6}} | collective-permute-start | bytes 19660808 | tf_op jit(solution)/shard_map/ppermute | solution.py:256
Sparse Core Ops, SparseCore 0:
  12.1 69.4 all-gather.16
  83.4 66.6 all-gather.18
  152.4 66.6 all-gather.8
  220.7 66.6 all-gather.10
  289.6 66.6 all-gather.12
  358.5 66.6 all-gather.14
  877.0 119.4 reduce-scatter.12
  999.6 119.3 reduce-scatter.6
  1260.3 119.3 reduce-scatter.14
  1382.7 119.3 reduce-scatter.8
  1578.1 119.4 reduce-scatter.16
  1700.6 119.3 reduce-scatter.10
